TPU v7x, 32 devices: a whole 2x2x4 slice. The times are simulated.
32 devices in a mesh: rep: 2 (over x), tp: 4 (over z), sp: 4 (over y, core).
Axes of the slice: x: 2, y: 2, z: 4, core: 2. Of those that a mesh axis runs over, the one named last changes fastest.
Arguments:
- x_tokens: bfloat16 [8192, 2560], P(('rep', 'sp')), parts along dimension 0
- positions: int32 [8192], P(('rep', 'sp')), parts along dimension 0
- gains: float32 [2, 4, 2560], replicated
- w_q: bfloat16 [2, 2560, 32, 128], P(None, None, 'tp')
- w_k: bfloat16 [2, 2560, 8, 128], P(None, None, 'tp')
- w_v: bfloat16 [2, 2560, 8, 128], P(None, None, 'tp')
- w_o: bfloat16 [2, 32, 128, 2560], P(None, 'tp')
- w_gate: bfloat16 [2, 2560, 9728], P(None, None, 'tp')
- w_up: bfloat16 [2, 2560, 9728], P(None, None, 'tp')
- w_down: bfloat16 [2, 9728, 2560], P(None, 'tp')
Outputs:
- output 1: bfloat16 [8192, 2560], P(('rep', 'sp')), parts along dimension 0
- output 2: bfloat16 [1024, 16, 128], P('rep', ('tp', 'sp')), parts along dimension 0
- output 3: bfloat16 [1024, 16, 128], P('rep', ('tp', 'sp')), parts along dimension 0
- output 4: bfloat16 [8192, 16, 128], P('rep', ('tp', 'sp')), parts along dimension 0
- output 5: bfloat16 [8192, 16, 128], P('rep', ('tp', 'sp')), parts along dimension 0
There are 2 independent parts. A program takes and returns all parts, laid end to end along the dimension named above; an argument that names none is the same for every part.
All inputs are finite; a program needn't handle non-finite values.
Results may differ from a plain program's by a relative error of at most 0.0160804.
Values are sent between devices in bfloat16 or wider.
A program may use at most 1 GiB of HBM per device.

v0:
```python
import jax
import jax.numpy as jnp
from jax import lax
from jax.sharding import PartitionSpec as P, NamedSharding

NORM_EPS = 1e-6
WINDOW = 512
Q_BLOCK = 256
LOCAL_BASE = 10000.0
GLOBAL_BASE = 1000000.0


def rms_norm(values, gain):
    wide = values.astype(jnp.float32)
    inv_rms = lax.rsqrt(jnp.mean(wide * wide, axis=-1, keepdims=True) + NORM_EPS)
    return wide * inv_rms * gain


def rotary(projected, positions, base):
    half = projected.shape[-1] // 2
    inv_freq = base ** (-jnp.arange(half, dtype=jnp.float32) / half)
    angles = positions.astype(jnp.float32)[..., None] * inv_freq
    cos_part = jnp.cos(angles)[..., None, :]
    sin_part = jnp.sin(angles)[..., None, :]
    first = projected[..., :half]
    second = projected[..., half:]
    return jnp.concatenate([first * cos_part - second * sin_part, second * cos_part + first * sin_part], axis=-1)


def attend(q_heads, k_heads, v_heads, q_first, local):
    total = k_heads.shape[0]
    span = WINDOW + Q_BLOCK if local else total
    scale = q_heads.shape[-1] ** -0.5

    def one_block(block_id):
        q_start = block_id * Q_BLOCK
        q_tile = lax.dynamic_slice_in_dim(q_heads, q_start, Q_BLOCK, 0)
        q_idx = q_first + q_start + jnp.arange(Q_BLOCK)
        k_start = jnp.clip(q_first + q_start - WINDOW, 0, total - span) if local else 0
        k_tile = lax.dynamic_slice_in_dim(k_heads, k_start, span, 0)
        v_tile = lax.dynamic_slice_in_dim(v_heads, k_start, span, 0)
        k_idx = k_start + jnp.arange(span)
        allowed = k_idx[None, :] <= q_idx[:, None]
        if local:
            allowed = allowed & (q_idx[:, None] - k_idx[None, :] < WINDOW)
        scores = jnp.einsum('qhgd,khd->hgqk', q_tile, k_tile, preferred_element_type=jnp.float32) * scale
        weights = jax.nn.softmax(jnp.where(allowed, scores, -1e30), axis=-1).astype(jnp.bfloat16)
        return jnp.einsum('hgqk,khd->qhgd', weights, v_tile, preferred_element_type=jnp.float32).astype(jnp.bfloat16)

    blocks = lax.map(one_block, jnp.arange(q_heads.shape[0] // Q_BLOCK))
    return blocks.reshape(q_heads.shape)


def solution(mesh):
    sp_size = mesh.shape['sp']

    def layer(x_loc, pos_loc, gain, w_q, w_k, w_v, w_o, w_gate, w_up, w_down, local):
        base = LOCAL_BASE if local else GLOBAL_BASE
        u_norm = rms_norm(x_loc, gain[0]).astype(jnp.bfloat16)
        q_rot = rotary(jnp.einsum('td,dhe->the', u_norm, w_q, preferred_element_type=jnp.float32), pos_loc, base).astype(jnp.bfloat16)
        k_rot = rotary(jnp.einsum('td,dhe->the', u_norm, w_k, preferred_element_type=jnp.float32), pos_loc, base).astype(jnp.bfloat16)
        v_new = jnp.einsum('td,dhe->the', u_norm, w_v, preferred_element_type=jnp.float32).astype(jnp.bfloat16)
        seq_dev, heads_tp, head_dim = q_rot.shape
        kv_tp = k_rot.shape[1]
        heads_dev = heads_tp // sp_size
        cache_dev = max(kv_tp // sp_size, 1)
        repeat = sp_size * cache_dev // kv_tp
        outgoing = jnp.concatenate([
            q_rot.reshape(seq_dev, sp_size, heads_dev, head_dim),
            jnp.repeat(k_rot, repeat, axis=1).reshape(seq_dev, sp_size, cache_dev, head_dim),
            jnp.repeat(v_new, repeat, axis=1).reshape(seq_dev, sp_size, cache_dev, head_dim)], axis=2)
        received = lax.all_to_all(outgoing, 'sp', 1, 0, tiled=True)
        total = received.shape[0]
        received = received.reshape(total, heads_dev + 2 * cache_dev, head_dim)
        q_all = received[:, :heads_dev].reshape(total, cache_dev, heads_dev // cache_dev, head_dim)
        k_all = received[:, heads_dev:heads_dev + cache_dev]
        v_all = received[:, heads_dev + cache_dev:]
        attn_out = attend(q_all, k_all, v_all, 0, local).reshape(sp_size, seq_dev, heads_dev, head_dim)
        attn_back = lax.all_to_all(attn_out, 'sp', 0, 2, tiled=True).reshape(seq_dev, heads_tp, head_dim)
        o_sum = lax.psum(jnp.einsum('the,hed->td', attn_back, w_o, preferred_element_type=jnp.float32), 'tp')
        x_mid = (x_loc.astype(jnp.float32) + rms_norm(o_sum, gain[1])).astype(jnp.bfloat16)
        u_mlp = rms_norm(x_mid, gain[2]).astype(jnp.bfloat16)
        gate_pre = jnp.dot(u_mlp, w_gate, preferred_element_type=jnp.float32)
        up_pre = jnp.dot(u_mlp, w_up, preferred_element_type=jnp.float32)
        hidden_act = (jax.nn.silu(gate_pre) * up_pre).astype(jnp.bfloat16)
        m_sum = lax.psum(jnp.dot(hidden_act, w_down, preferred_element_type=jnp.float32), 'tp')
        x_out = (x_mid.astype(jnp.float32) + rms_norm(m_sum, gain[3])).astype(jnp.bfloat16)
        if local:
            return x_out, k_all[total - WINDOW:], v_all[total - WINDOW:]
        return x_out, k_all, v_all

    def device_fn(x_loc, pos_loc, gains, w_q, w_k, w_v, w_o, w_gate, w_up, w_down):
        hidden, k_local, v_local = layer(x_loc, pos_loc, gains[0], w_q[0], w_k[0], w_v[0], w_o[0], w_gate[0], w_up[0], w_down[0], True)
        out_hidden, k_global, v_global = layer(hidden, pos_loc, gains[1], w_q[1], w_k[1], w_v[1], w_o[1], w_gate[1], w_up[1], w_down[1], False)
        return out_hidden, k_local, v_local, k_global, v_global

    token_spec = P(('rep', 'sp'), None)
    cache_spec = P('rep', ('tp', 'sp'), None)
    in_specs = (token_spec, P(('rep', 'sp')), P(), P(None, None, 'tp', None), P(None, None, 'tp', None),
                P(None, None, 'tp', None), P(None, 'tp', None, None), P(None, None, 'tp'), P(None, None, 'tp'),
                P(None, 'tp', None))
    out_specs = (token_spec, cache_spec, cache_spec, cache_spec, cache_spec)
    return jax.shard_map(device_fn, mesh=mesh, in_specs=in_specs, out_specs=out_specs, check_vma=False)
```

profile of v0, /device:TPU:0, one launch (start us, length us, event | category | flops | bytes accessed | tf_op | source)
XLA Modules:
  0.0 2125.3 jit_solution(5889949905492592512)
XLA Ops:
  8.0 3.6 fusion.47
  12.4 2.8 fusion.116
  16.2 4.6 fusion.117
  20.8 5.2 fusion.103
  27.8 9.0 fusion.112
  36.8 8.2 copy.68
  44.9 9.4 fusion.105
  54.3 2.7 multiply_cosine_fusion
  58.2 2.2 pad_maximum_fusion
  60.5 16.4 all-to-all-start
  76.9 48.5 %all-to-all-done = bf16[1024,4,4,128]{0,3,2,1:T(8,128)(2,1)} async-done(((bf16[1024,4,4,128]{0,3,2,1:T(8,128)(2,1)}), bf16[1024,4,4,128]{0,3,2,1:T(8,128)(2,1)}, u32[]{:S(2)}, u32[]{:S(2)}) %all-to-all-start) | async-done | bytes 4194336 | tf_op jit(solution)/shard_map/all_to_all | solution.py:72
  125.5 6.2 copy.50
  131.7 3.2 slice_bitcast_fusion.1
  136.5 74.2 %while.22 = (s32[]{:T(128)}, bf16[16,256,1,2,128]{4,1,0,3,2:T(8,128)(2,1)S(1)}, s32[16]{0:T(128)S(1)}, bf16[4096,1,128]{2,0,1:T(8,128)(2,1)}, bf16[4096,1,128]{2...) while((s32[]{:T(128)}, ...), condition=%wide.region_4.5_spmd, body=%wide.region_1.4_spmd.sunk | while | flops 205324288 | bytes 6310131 | solution.py:50
  210.8 28.1 %all_to_all.60 = bf16[4,1024,2,128]{3,1,2,0:T(8,128)(2,1)S(1)} all-to-all(bf16[4,1024,2,128]{3,1,2,0:T(8,128)(2,1)S(1)} %copy.54), channel_id=1, replica_groups=mesh['rep'=2,'tp'=4,'sp'=4] {'sp'}, dimensions={0} | all-to-all | bytes 4194304 | tf_op jit(solution)/shard_map/all_to_all | solution.py:79
  238.9 9.9 convolution_bitcast_fusion.1
  248.9 357.7 %all-reduce.5.cloned.1.call-done = f32[1024,2560]{1,0:T(8,128)} async-done(((f32[1024,2560]{1,0:T(8,128)}), f32[1024,2560]{1,0:T(8,128)}) %all-reduce.5.cloned.1.call-update) | async-done | bytes 10485776 | tf_op jit(solution)/shard_map/psum | solution.py:80
  606.6 4.7 multiply_reduce_fusion.3
  611.3 10.1 fusion.51
  621.4 20.8 fusion.39
  642.2 20.4 multiply_convert_fusion.1.clone.5
  662.6 20.8 fusion.35
  685.7 8.1 copy.71
  693.8 345.2 %all-reduce.7.cloned.1.call-done = f32[1024,2560]{1,0:T(8,128)} async-done(((f32[1024,2560]{1,0:T(8,128)}), f32[1024,2560]{1,0:T(8,128)}) %all-reduce.7.cloned.1.call-update) | async-done | bytes 10485776 | tf_op jit(solution)/shard_map/psum | solution.py:86
  1039.0 4.7 multiply_reduce_fusion.2
  1043.7 10.2 fusion.55
  1054.0 11.2 fusion.100
  1066.8 2.8 fusion.98
  1071.2 2.9 subtract_convert_fusion
  1074.4 2.2 pad_maximum_fusion.1
  1076.7 4.9 all-to-all-start.2
  1081.6 47.8 %all-to-all-done.2 = bf16[1024,4,4,128]{0,3,2,1:T(8,128)(2,1)} async-done(((bf16[1024,4,4,128]{0,3,2,1:T(8,128)(2,1)}), bf16[1024,4,4,128]{0,3,2,1:T(8,128)(2,1)}, u32[]{:S(2)}, u32[]{:S(2)}) %all-to-all-start.2) | async-done | bytes 4194336 | tf_op jit(solution)/shard_map/all_to_all | solution.py:72
  1129.4 6.3 copy.59
  1135.7 3.2 slice_bitcast_fusion
  1140.5 137.4 %while.23 = (s32[]{:T(128)}, bf16[16,256,1,2,128]{4,1,0,3,2:T(8,128)(2,1)S(1)}, s32[16]{0:T(128)S(1)}, bf16[4096,1,2,128]{3,0,2,1:T(8,128)(2,1)}, bf16[4096,1,12...) while((s32[]{:T(128)}, ...), condition=%wide.region_14.15_spmd, body=%wide.region_11.14_spmd.sunk | while | flops 1091632384 | bytes 29634740 | solution.py:50
  1142.4 3.2 fusion.167
  1146.9 2.1 fusion.169
  1151.0 3.2 fusion.167
  1155.5 2.1 fusion.169
  1159.6 3.2 fusion.167
  1168.2 3.2 fusion.167
  1176.8 3.2 fusion.167
  1185.4 3.2 fusion.167
  1194.0 3.2 fusion.167
  1202.6 3.2 fusion.167
  1211.2 3.2 fusion.167
  1219.8 3.2 fusion.167
  1228.3 3.2 fusion.167
  1236.9 3.2 fusion.167
  1245.5 3.2 fusion.167
  1254.1 3.2 fusion.167
  1262.7 3.2 fusion.167
  1271.3 3.2 fusion.167
  1278.1 28.3 %all_to_all.61 = bf16[4,1024,2,128]{3,1,2,0:T(8,128)(2,1)S(1)} all-to-all(bf16[4,1024,2,128]{3,1,2,0:T(8,128)(2,1)S(1)} %copy.61), channel_id=1, replica_groups=mesh['rep'=2,'tp'=4,'sp'=4] {'sp'}, dimensions={0} | all-to-all | bytes 4194304 | tf_op jit(solution)/shard_map/all_to_all | solution.py:79
  1306.4 9.9 convolution_bitcast_fusion
  1316.4 354.6 %all-reduce.9.cloned.1.call-done = f32[1024,2560]{1,0:T(8,128)} async-done(((f32[1024,2560]{1,0:T(8,128)}), f32[1024,2560]{1,0:T(8,128)}) %all-reduce.9.cloned.1.call-update) | async-done | bytes 10485776 | tf_op jit(solution)/shard_map/psum | solution.py:80
  1671.0 4.7 multiply_reduce_fusion.1
  1675.7 10.1 fusion.59
  1685.9 20.8 fusion.33
  1706.6 20.4 multiply_convert_fusion.clone.5
  1727.1 20.6 fusion.29
  1749.4 353.9 %all-reduce.11.cloned.1.call-done = f32[1024,2560]{1,0:T(8,128)} async-done(((f32[1024,2560]{1,0:T(8,128)}), f32[1024,2560]{1,0:T(8,128)}) %all-reduce.11.cloned.1.call-update) | async-done | bytes 10485776 | tf_op jit(solution)/shard_map/psum | solution.py:86
  2103.3 4.7 multiply_reduce_fusion
  2108.1 10.2 fusion.62
  (306 shorter events, 150.3 us)
Async XLA Ops:
  7.2 4.5 copy-start.12
  7.2 5.3 copy-start.6
  16.2 9.8 slice-start
  20.8 5.2 slice-start.1
  44.9 12.1 copy-start.10
  60.5 65.0 %all-to-all-start = ((bf16[1024,4,4,128]{0,3,2,1:T(8,128)(2,1)}), bf16[1024,4,4,128]{0,3,2,1:T(8,128)(2,1)}, u32[]{:S(2)}, u32[]{:S(2)}) async-start(bf16[1024,4,4,128]{0,3,2,1:T(8,128)(2,1)} %pad_maximum_fusion), calls=%async_computation | async-start | bytes 8388608 | tf_op jit(solution)/shard_map/all_to_all | solution.py:72
  76.9 529.7 %all-reduce.5.cloned.1.call-start = ((), (), s32[]{:S(2)}) async-start(), calls=%async_computation.4 | async-start | bytes 20971520 | tf_op jit(solution)/shard_map/psum | solution.py:80
  131.7 3.2 copy-start.3
  248.8 790.1 %all-reduce.7.cloned.1.call-start = ((), (), s32[]{:S(2)}) async-start(), calls=%async_computation.5 | async-start | bytes 20971520 | tf_op jit(solution)/shard_map/psum | solution.py:86
  621.4 20.8 copy-start.1
  683.4 1.3 copy-start.5
  693.7 350.0 %copy-start.15 = (f32[2560]{0:T(1024)S(1)}, f32[2560]{0:T(1024)}, u32[]{:S(2)}) copy-start(f32[2560]{0:T(1024)} %get-tuple-element.137) | copy-start | bytes 30724
  1043.7 10.2 copy-start.17
  1053.9 11.2 copy-start
  1053.9 11.2 copy-start.9
  1066.8 3.0 copy-start.7
  1066.8 3.0 copy-start.8
  1076.7 52.7 %all-to-all-start.2 = ((bf16[1024,4,4,128]{0,3,2,1:T(8,128)(2,1)}), bf16[1024,4,4,128]{0,3,2,1:T(8,128)(2,1)}, u32[]{:S(2)}, u32[]{:S(2)}) async-start(bf16[1024,4,4,128]{0,3,2,1:T(8,128)(2,1)} %pad_maximum_fusion.1), calls=%async_computation.2 | async-start | bytes 8388608 | tf_op jit(solution)/shard_map/all_to_all | solution.py:72
  1081.5 589.5 %all-reduce.9.cloned.1.call-start = ((), (), s32[]{:S(2)}) async-start(), calls=%async_computation.6 | async-start | bytes 20971520 | tf_op jit(solution)/shard_map/psum | solution.py:80
  1135.7 3.2 copy-start.4
  1277.9 38.4 %copy-start.11 = (bf16[4096,1,128]{2,0,1:T(8,128)(2,1)}, bf16[4096,1,128]{2,0,1:T(8,128)(2,1)S(1)}, u32[]{:S(2)}) copy-start(bf16[4096,1,128]{2,0,1:T(8,128)(2,1)S(1)} %get-tuple-element.372) | copy-start | bytes 3145732
  1316.3 359.4 %copy-start.14 = (f32[2560]{0:T(1024)S(1)}, f32[2560]{0:T(1024)}, u32[]{:S(2)}) copy-start(f32[2560]{0:T(1024)} %get-tuple-element.135) | copy-start | bytes 30724
  1316.4 787.0 %all-reduce.11.cloned.1.call-start = ((), (), s32[]{:S(2)}) async-start(), calls=%async_computation.7 | async-start | bytes 20971520 | tf_op jit(solution)/shard_map/psum | solution.py:86
  1675.7 10.1 copy-start.16
  1685.9 20.8 copy-start.2
  1749.4 358.6 %copy-start.13 = (f32[2560]{0:T(1024)S(1)}, f32[2560]{0:T(1024)}, u32[]{:S(2)}) copy-start(f32[2560]{0:T(1024)} %get-tuple-element.134) | copy-start | bytes 30724
Sparse Core Ops, SparseCore 0:
  249.0 357.5 all-reduce.4
  683.5 355.4 all-reduce.6
  1316.5 354.4 all-reduce.8
  1747.9 355.4 all-reduce.10
where the time goes:
time: 2130 us
  waiting for transfers between devices  1510 us (71%)
  matrix products  305 us (14%)
  other arithmetic  115 us (5%)
  local copies, waits for them, and re-layouts  82.8 us (4%)
  blocking collectives  56.5 us (3%)
  loops' own time  22.2 us (1%)
  starting transfers between devices  21.4 us (1%)
    psum x2, waiting for transfers between devices, layer(): lax.psum(jnp.einsum('the,hed->td', attn_back, w_o, preferred_element_type...  712 us
    psum x2, waiting for transfers between devices, layer(): lax.psum(jnp.dot(hidden_act, w_down, preferred_element_type=jnp.float32),...  699 us
    all_to_all x2, waiting for transfers between devices, layer(): received = lax.all_to_all(outgoing, 'sp', 1, 0, tiled=True)  96.4 us
    dot_general x32, matrix products, one_block(): jnp.einsum('qhgd,khd->hgqk', q_tile, k_tile, preferred_element_type=jnp.f...  72.7 us
    dot_general x32, matrix products, one_block(): jnp.einsum('hgqk,khd->qhgd', weights, v_tile, preferred_element_type=jnp....  56.7 us
    all_to_all x2, blocking collectives, layer(): lax.all_to_all(attn_out, 'sp', 0, 2, tiled=True)  56.5 us
    reduce_sum x8, other arithmetic, rms_norm(): jnp.mean(wide * wide, axis=-1, keepdims=True) + NORM_EPS  52.9 us
  transfers between devices with their start and end apart: 6, of which 6 were waited for; matrix products, arithmetic and copies ran while one was open for 1% of the time, Pallas kernels for 0%

commit v1 on v0

v1 whole, which is shorter than its diff:
```python
import functools
import jax
import jax.numpy as jnp
from jax import lax
from jax.experimental import pallas as pl
from jax.experimental.pallas import tpu as pltpu
from jax.sharding import PartitionSpec as P

MESH = pl.DeviceIdType.MESH
NORM_EPS = 1e-6
D = 2560
WINDOW = 512
QB = 256
LOG2E = 1.4426950408889634
NT = (((1,), (1,)), ((), ()))

def attn_kernel(local, x_hbm, g_ref, cos_ref, sin_ref, wkv_hbm, wq_hbm, a_hbm, kc_hbm, vc_hbm,
                x_v, wkv_v, wq_v, q_v, kv, cache, m_v, l_v, acc_v, a_v,
                w_sem, ps_sem, pr_sem, ys_sem, yr_sem, fs_sem, fr_sem, c_sem):
    s = lax.axis_index('sp')
    rows = x_v.shape[0]
    nq = rows // QB
    y = s // 2
    pair = {'sp': s + 1 - 2 * lax.rem(s, 2)}
    across = {'sp': lax.rem(s + 2, 4)}
    loads = [pltpu.make_async_copy(x_hbm, x_v, w_sem.at[0]), pltpu.make_async_copy(wkv_hbm, wkv_v, w_sem.at[1]),
             pltpu.make_async_copy(wq_hbm, wq_v, w_sem.at[2])]
    for c in loads:
        c.start()
    bar = pltpu.get_barrier_semaphore()
    if local:
        own = WINDOW

        @pl.when(s > 0)
        def _():
            pl.semaphore_signal(bar, inc=1, device_id={'sp': jnp.maximum(s - 1, 0)}, device_id_type=MESH)

        @pl.when(s < 3)
        def _():
            pl.semaphore_signal(bar, inc=1, device_id={'sp': 3}, device_id_type=MESH)
        pl.semaphore_wait(bar, jnp.where(s == 3, 3, 1))
    else:
        own = pl.multiple_of(s * rows, rows)
        for peer in (pair, across):
            pl.semaphore_signal(bar, inc=1, device_id=peer, device_id_type=MESH)
        pl.semaphore_wait(bar, 2)

    def halo():
        return pltpu.make_async_remote_copy(kv.at[:, pl.ds(rows, WINDOW), :], kv.at[:, pl.ds(0, WINDOW), :],
                                            ps_sem.at[0], pr_sem.at[0], device_id={'sp': jnp.minimum(s + 1, 3)}, device_id_type=MESH)

    def tail(dst, kind):
        return pltpu.make_async_remote_copy(kv.at[2 * kind + dst // 2, pl.ds(rows, WINDOW), :], cache.at[kind],
                                            ys_sem.at[dst, kind], yr_sem.at[kind], device_id={'sp': dst}, device_id_type=MESH)

    def region(b):
        return kv.at[:, pl.ds(pl.multiple_of(own + b * QB, QB), QB), :]

    def to_pair(b):
        return pltpu.make_async_remote_copy(region(b), region(b), ps_sem.at[b], pr_sem.at[b], device_id=pair, device_id_type=MESH)

    def to_across(b):
        return pltpu.make_async_remote_copy(region(b), region(b), ys_sem.at[b], yr_sem.at[b], device_id=across, device_id_type=MESH)

    def fwd(b):
        ref = kv.at[:, pl.ds(pl.multiple_of(lax.rem(s + 2, 4) * rows + b * QB, QB), QB), :]
        return pltpu.make_async_remote_copy(ref, ref, fs_sem.at[b], fr_sem.at[b], device_id=pair, device_id_type=MESH)

    def rope(v, rs):
        return v * cos_ref[rs, :] + pltpu.roll(v, 64, 1) * sin_ref[rs, :]

    loads[0].wait()
    loads[1].wait()

    def kv_block(k, _):
        b = lax.rem(k + 2, nq) if local else k
        rs = pl.ds(pl.multiple_of(b * QB, QB), QB)
        wide = x_v[rs, :].astype(jnp.float32)
        u = (wide * lax.rsqrt(jnp.mean(wide * wide, axis=-1, keepdims=True) + NORM_EPS) * g_ref[0:1, :]).astype(jnp.bfloat16)
        x_v[rs, :] = u
        p = jnp.dot(u, wkv_v[...], preferred_element_type=jnp.float32)
        dst = pl.ds(pl.multiple_of(own + b * QB, QB), QB)
        for h in range(2):
            kv[h, dst, :] = rope(p[:, h * 128:(h + 1) * 128], rs).astype(jnp.bfloat16)
            kv[2 + h, dst, :] = p[:, (2 + h) * 128:(3 + h) * 128].astype(jnp.bfloat16)
        if local:
            @pl.when(k == 1)
            def _():
                @pl.when(s < 3)
                def _():
                    halo().start()

                @pl.when(s == 3)
                def _():
                    for dst in range(3):
                        for kind in range(2):
                            tail(dst, kind).start()
        else:
            to_across(b).start()
            to_pair(b).start()
        return 0
    lax.fori_loop(0, nq, kv_block, 0)

    loads[2].wait()

    def q_block(b, _):
        rs = pl.ds(pl.multiple_of(b * QB, QB), QB)
        for g in range(2):
            for hh in range(2):
                p = jnp.dot(x_v[rs, :], wq_v[:, (g * 4 + hh * 2) * 128:(g * 4 + hh * 2 + 2) * 128], preferred_element_type=jnp.float32)
                for e in range(2):
                    q_v[g, b, hh, pl.ds(e * QB, QB), :] = rope(p[:, e * 128:(e + 1) * 128], rs).astype(jnp.bfloat16)
        return 0
    lax.fori_loop(0, nq, q_block, 0)

    scale = 128 ** -0.5 * LOG2E

    def scores(g, b, hh, ks):
        return lax.dot_general(q_v[g, b, hh], kv[g, ks, :], NT, preferred_element_type=jnp.float32) * scale

    def emit(g, b, hh, o):
        for e in range(2):
            a_v[pl.ds(pl.multiple_of(b * QB, QB), QB), pl.ds(pl.multiple_of((g * 4 + hh * 2 + e) * 128, 128), 128)] = o[e * QB:(e + 1) * QB]

    def tiles(fn):
        def body(k, _):
            fn(k // (2 * nq), lax.rem(k // 2, nq), lax.rem(k, 2))
            return 0
        lax.fori_loop(0, 4 * nq, body, 0)

    if local:
        @pl.when(s > 0)
        def _():
            halo().wait_recv()

        @pl.when(s == 0)
        def _():
            kv[:, :WINDOW, :] = jnp.zeros((4, WINDOW, 128), jnp.bfloat16)

        def tile(g, b, hh):
            span = WINDOW + QB
            ks = pl.ds(pl.multiple_of(b * QB, QB), span)
            sc = scores(g, b, hh, ks)
            i = lax.rem(lax.broadcasted_iota(jnp.int32, sc.shape, 0), QB)
            j = lax.broadcasted_iota(jnp.int32, sc.shape, 1)
            first = jnp.where(s == 0, WINDOW - b * QB, 0)
            ok = (j > i) & (j <= i + WINDOW) & (j >= first)
            sc = jnp.where(ok, sc, -1e30)
            p = jnp.exp2(sc - jnp.max(sc, axis=1, keepdims=True))
            o = jnp.dot(p.astype(jnp.bfloat16), kv[2 + g, ks, :], preferred_element_type=jnp.float32)
            emit(g, b, hh, (o / jnp.sum(p, axis=1, keepdims=True)).astype(jnp.bfloat16))
        tiles(tile)

        @pl.when(s < 3)
        def _():
            halo().wait_send()
            for kind in range(2):
                tail(0, kind).wait_recv()

        @pl.when(s == 3)
        def _():
            for dst in range(3):
                for kind in range(2):
                    tail(dst, kind).wait_send()
            for kind in range(2):
                cache[kind] = kv[2 * kind + 1, pl.ds(rows, WINDOW), :]
        outs = [pltpu.make_async_copy(a_v, a_hbm, c_sem.at[0]), pltpu.make_async_copy(cache.at[0], kc_hbm, c_sem.at[1]),
                pltpu.make_async_copy(cache.at[1], vc_hbm, c_sem.at[2])]
        for c in outs:
            c.start()
        for c in outs:
            c.wait()
        return

    def update(g, b, hh, ks, mask):
        sc = scores(g, b, hh, ks)
        if mask is not None:
            sc = jnp.where(mask(sc.shape), sc, -1e30)
        m_old = m_v[g, b, hh]
        m_new = jnp.maximum(m_old, jnp.max(sc, axis=1, keepdims=True))
        alpha = jnp.exp2(m_old - m_new)
        p = jnp.exp2(sc - jnp.concatenate([m_new] * (sc.shape[1] // 128), axis=1))
        part = p[:, :128]
        for c in range(1, sc.shape[1] // 128):
            part = part + p[:, c * 128:(c + 1) * 128]
        l_v[g, b, hh] = l_v[g, b, hh] * alpha + part
        acc_v[g, b, hh] = acc_v[g, b, hh] * alpha + jnp.dot(p.astype(jnp.bfloat16), kv[2 + g, ks, :], preferred_element_type=jnp.float32)
        m_v[g, b, hh] = m_new

    def diag(g, b, hh):
        m_v[g, b, hh] = jnp.full((2 * QB, 128), -1e30, jnp.float32)
        l_v[g, b, hh] = jnp.zeros((2 * QB, 128), jnp.float32)
        acc_v[g, b, hh] = jnp.zeros((2 * QB, 128), jnp.float32)

        def before(j, _):
            update(g, b, hh, pl.ds(pl.multiple_of(own + j * QB, QB), QB), None)
            return 0
        lax.fori_loop(0, b, before, 0)

        def mask(shape):
            return lax.broadcasted_iota(jnp.int32, shape, 1) <= lax.rem(lax.broadcasted_iota(jnp.int32, shape, 0), QB)
        update(g, b, hh, pl.ds(pl.multiple_of(own + b * QB, QB), QB), mask)
    tiles(diag)

    def full(src):
        def tile(g, b, hh):
            def blk(j, _):
                update(g, b, hh, pl.ds(pl.multiple_of(src * rows + j * 512, 512), 512), None)
                return 0
            lax.fori_loop(0, rows // 512, blk, 0)
        tiles(tile)

    def pass_on(b, _):
        to_across(b).wait_recv()
        fwd(b).start()
        return 0

    def wait_pair(b, _):
        to_pair(b).wait_recv()
        return 0

    def wait_fwd(b, _):
        fwd(b).wait_recv()
        return 0
    lax.fori_loop(0, nq, wait_pair, 0)

    @pl.when(lax.rem(s, 2) == 1)
    def _():
        full(s - 1)
    lax.fori_loop(0, nq, pass_on, 0)

    @pl.when(y == 1)
    def _():
        full(lax.rem(s + 2, 4))
    lax.fori_loop(0, nq, wait_fwd, 0)
    outs = [pltpu.make_async_copy(kv.at[y], kc_hbm, c_sem.at[1]), pltpu.make_async_copy(kv.at[2 + y], vc_hbm, c_sem.at[2])]
    for c in outs:
        c.start()

    @pl.when(y == 1)
    def _():
        full(1 - lax.rem(s, 2))

    def fin(g, b, hh):
        emit(g, b, hh, (acc_v[g, b, hh] / jnp.sum(l_v[g, b, hh], axis=1, keepdims=True)).astype(jnp.bfloat16))
    tiles(fin)
    last = pltpu.make_async_copy(a_v, a_hbm, c_sem.at[0])
    last.start()

    def sent(b, _):
        to_pair(b).wait_send()
        to_across(b).wait_send()
        fwd(b).wait_send()
        return 0
    lax.fori_loop(0, nq, sent, 0)
    for c in outs + [last]:
        c.wait()


def attn(local, x, gains, cos, sin, wkv, wq, cid):
    t = x.shape[0]
    nq = t // QB
    any_ = pl.BlockSpec(memory_space=pl.ANY)
    vm = pl.BlockSpec(memory_space=pltpu.VMEM)
    bf, f32 = jnp.bfloat16, jnp.float32
    dma = pltpu.SemaphoreType.DMA
    total = WINDOW if local else 4 * t
    kvrows = WINDOW + t if local else 4 * t
    st = (2, nq, 2, 2 * QB, 128) if not local else (1, 1, 1, 8, 128)
    return pl.pallas_call(
        functools.partial(attn_kernel, local),
        out_shape=[jax.ShapeDtypeStruct((t, 1024), bf), jax.ShapeDtypeStruct((total, 128), bf), jax.ShapeDtypeStruct((total, 128), bf)],
        in_specs=[any_, vm, vm, vm, any_, any_],
        out_specs=[any_, any_, any_],
        scratch_shapes=[
            pltpu.VMEM((t, D), bf), pltpu.VMEM((D, 512), bf), pltpu.VMEM((D, 1024), bf), pltpu.VMEM((2, nq, 2, 2 * QB, 128), bf),
            pltpu.VMEM((4, kvrows, 128), bf), pltpu.VMEM((2, WINDOW, 128), bf),
            pltpu.VMEM(st, f32), pltpu.VMEM(st, f32), pltpu.VMEM(st, f32), pltpu.VMEM((t, 1024), bf),
            dma((3,)), dma((nq,)), dma((nq,)), dma((3, 2)) if local else dma((nq,)), dma((2,)) if local else dma((nq,)),
            dma((nq,)), dma((nq,)), dma((3,))],
        compiler_params=pltpu.CompilerParams(collective_id=cid, has_side_effects=True, vmem_limit_bytes=60 * 2**20),
        cost_estimate=pl.CostEstimate(flops=20_000_000_000, bytes_accessed=20_000_000, transcendentals=10_000_000),
        name='attn_local' if local else 'attn_global',
    )(x, gains, cos, sin, wkv, wq)


def ffn_kernel(layer, C, a_hbm, h_hbm, g_ref, wo_hbm, wg_hbm, wu_hbm, wd_hbm, out_hbm,
               wo_v, wg_v, wu_v, wd_v, a_v, hb, ub, so, sm, ro, rm, lhs_a, lhs_u, fb,
               w_sem, os_sem, or_sem, ms_sem, mr_sem, us_sem, ur_sem, hs_sem, hr_sem, out_sem):
    z = lax.axis_index('tp')
    half = a_hbm.shape[0] // 2
    n = half // C
    q = ro.shape[1]
    ff = wg_v.shape[1]
    r = (z, 3 - z)
    toward = ({'tp': jnp.maximum(z - 1, 0)}, {'tp': jnp.minimum(z + 1, 3)})
    away = ({'tp': jnp.minimum(z + 1, 3)}, {'tp': jnp.maximum(z - 1, 0)})

    def load(k, src, dst):
        return pltpu.make_async_copy(src, dst, w_sem.at[k])

    is_end = (z == 0) | (z == 3)
    loads = [load(0, wo_hbm.at[layer], wo_v), load(1, a_hbm, a_v), load(2, wg_hbm.at[layer], wg_v),
             load(3, wu_hbm.at[layer], wu_v), load(4, wd_hbm.at[layer], wd_v)]
    res = load(5, h_hbm.at[pl.ds(pl.multiple_of(jnp.where(z == 3, half, 0), half), half), :], hb)
    for c in loads[:2]:
        c.start()

    @pl.when(is_end)
    def _():
        res.start()
    for c in loads[2:]:
        c.start()

    bar = pltpu.get_barrier_semaphore()

    @pl.when(z > 0)
    def _():
        pl.semaphore_signal(bar, inc=1, device_id={'tp': jnp.maximum(z - 1, 0)}, device_id_type=MESH)

    @pl.when(z < 3)
    def _():
        pl.semaphore_signal(bar, inc=1, device_id={'tp': jnp.minimum(z + 1, 3)}, device_id_type=MESH)
    pl.semaphore_wait(bar, jnp.where(is_end, 1, 2))

    for c in loads[:2]:
        c.wait()

    @pl.when(is_end)
    def _():
        res.wait()

    def rms(v, gain):
        return v * lax.rsqrt(jnp.mean(v * v, axis=-1, keepdims=True) + NORM_EPS) * gain

    def red_copy(stage, recv, s_sem, r_sem, d, slot, i):
        k = lax.rem(i, q)
        return pltpu.make_async_remote_copy(stage.at[slot, d], recv.at[d, k], s_sem.at[slot, d], r_sem.at[d, k],
                                            device_id=toward[d], device_id_type=MESH)

    def cast_copy(s_sem, r_sem, d, i):
        return pltpu.make_async_remote_copy(ub.at[d, i], ub.at[d, i], s_sem.at[d, i], r_sem.at[d, i],
                                            device_id=away[d], device_id_type=MESH)

    def out_copy(d, i):
        return pltpu.make_async_copy(ub.at[d, i], out_hbm.at[pl.ds(pl.multiple_of(d * half + i * C, C), C), :], out_sem.at[d, i])

    def tick(t, _):
        slot = lax.rem(t, 2)

        def free_stage(stage, recv, s_sem, r_sem, first):
            for d in (0, 1):
                i = t - first - 3 + r[d] - 2

                @pl.when((i >= 0) & (i < n) & (r[d] > 0))
                def _():
                    red_copy(stage, recv, s_sem, r_sem, d, slot, i).wait_send()

        def reduce(stage, recv, s_sem, r_sem, first, at_end):
            for d in (0, 1):
                i = t - first - 3 + r[d]
                act = (i >= 0) & (i < n)

                @pl.when(act & (r[d] < 3))
                def _():
                    red_copy(stage, recv, s_sem, r_sem, d, slot, i).wait_recv()
                    stage[slot, d] += recv[d, lax.rem(i, q)]

                @pl.when(act & (r[d] > 0))
                def _():
                    red_copy(stage, recv, s_sem, r_sem, d, slot, i).start()

                @pl.when(act & (r[d] == 0))
                def _():
                    at_end(d, i)

        def spread(s_sem, r_sem, first, then):
            for d in (0, 1):
                i = t - first - r[d]
                act = (i >= 0) & (i < n) & (r[d] > 0)

                @pl.when(act)
                def _():
                    cast_copy(s_sem, r_sem, d, i).wait_recv()

                @pl.when(act & (r[d] < 3))
                def _():
                    cast_copy(s_sem, r_sem, d, i).start()
                if then is not None:
                    @pl.when(act)
                    def _():
                        then(d, i)

        free_stage(so, ro, os_sem, or_sem, 0)

        @pl.when(t < n + 3)
        def _():
            for d in (0, 1):
                i = jnp.clip(t - 3 + r[d], 0, n - 1)
                lhs_a[pl.ds(d * C, C), :] = a_v[pl.ds(pl.multiple_of(d * half + i * C, C), C), :]

            def cols(j, _):
                cs = pl.ds(pl.multiple_of(j * 256, 256), 256)
                p = jnp.dot(lhs_a[...], wo_v[:, cs], preferred_element_type=jnp.float32)
                so[slot, 0, :, cs] = p[:C]
                so[slot, 1, :, cs] = p[C:]
                return 0
            lax.fori_loop(0, D // 256, cols, 0)

        def o_end(d, i):
            rows = pl.ds(pl.multiple_of(i * C, C), C)
            h1 = (hb[rows, :].astype(jnp.float32) + rms(so[slot, d], g_ref[1:2, :])).astype(jnp.bfloat16)
            hb[rows, :] = h1
            ub[d, i] = rms(h1.astype(jnp.float32), g_ref[2:3, :]).astype(jnp.bfloat16)
            cast_copy(us_sem, ur_sem, d, i).start()
        reduce(so, ro, os_sem, or_sem, 0, o_end)
        spread(us_sem, ur_sem, 3, None)

        @pl.when(t == 6)
        def _():
            for c in loads[2:]:
                c.wait()
        free_stage(sm, rm, ms_sem, mr_sem, 6)

        @pl.when((t >= 6) & (t < n + 9))
        def _():
            for d in (0, 1):
                i = t - 9 + r[d]

                @pl.when((i >= 0) & (i < n) & (r[d] < 3))
                def _():
                    cast_copy(us_sem, ur_sem, d, i).wait_send()

                @pl.when((i >= 0) & (i < n))
                def _():
                    lhs_u[pl.ds(d * C, C), :] = ub[d, jnp.clip(i, 0, n - 1)]

            def hidden(cs):
                gate = jnp.dot(lhs_u[...], wg_v[:, cs], preferred_element_type=jnp.float32)
                up = jnp.dot(lhs_u[...], wu_v[:, cs], preferred_element_type=jnp.float32)
                fb[:, cs] = (gate / (1.0 + jnp.exp(-gate)) * up).astype(jnp.bfloat16)

            def hcols(j, _):
                hidden(pl.ds(pl.multiple_of(j * 256, 256), 256))
                return 0
            lax.fori_loop(0, ff // 256, hcols, 0)
            if ff % 256:
                hidden(pl.ds(ff // 256 * 256, ff % 256))

            def dcols(j, _):
                cs = pl.ds(pl.multiple_of(j * 256, 256), 256)
                p = jnp.dot(fb[...], wd_v[:, cs], preferred_element_type=jnp.float32)
                sm[slot, 0, :, cs] = p[:C]
                sm[slot, 1, :, cs] = p[C:]
                return 0
            lax.fori_loop(0, D // 256, dcols, 0)

        def m_end(d, i):
            rows = pl.ds(pl.multiple_of(i * C, C), C)
            ub[d, i] = (hb[rows, :].astype(jnp.float32) + rms(sm[slot, d], g_ref[3:4, :])).astype(jnp.bfloat16)
            cast_copy(hs_sem, hr_sem, d, i).start()
            out_copy(d, i).start()
        reduce(sm, rm, ms_sem, mr_sem, 6, m_end)
        spread(hs_sem, hr_sem, 9, lambda d, i: out_copy(d, i).start())
        return 0

    lax.fori_loop(0, n + 12, tick, 0)

    def drain(i, _):
        for d in (0, 1):
            @pl.when(r[d] < 3)
            def _():
                cast_copy(hs_sem, hr_sem, d, i).wait_send()
            out_copy(d, i).wait()
        return 0
    lax.fori_loop(0, n, drain, 0)


def ffn(layer, a, h, gains, w_o, w_gate, w_up, w_down, C=32, q=4, cid=0):
    t, ka = a.shape
    ff = w_gate.shape[-1]
    n = t // 2 // C
    any_ = pl.BlockSpec(memory_space=pl.ANY)
    bf, f32 = jnp.bfloat16, jnp.float32
    dma = pltpu.SemaphoreType.DMA
    return pl.pallas_call(
        functools.partial(ffn_kernel, layer, C),
        out_shape=jax.ShapeDtypeStruct((t, D), bf),
        in_specs=[any_, any_, pl.BlockSpec(memory_space=pltpu.VMEM), any_, any_, any_, any_],
        out_specs=any_,
        scratch_shapes=[
            pltpu.VMEM((ka, D), bf), pltpu.VMEM((D, ff), bf), pltpu.VMEM((D, ff), bf), pltpu.VMEM((ff, D), bf),
            pltpu.VMEM((t, ka), bf), pltpu.VMEM((t // 2, D), bf), pltpu.VMEM((2, n, C, D), bf),
            pltpu.VMEM((2, 2, C, D), f32), pltpu.VMEM((2, 2, C, D), f32),
            pltpu.VMEM((2, q, C, D), f32), pltpu.VMEM((2, q, C, D), f32),
            pltpu.VMEM((2 * C, ka), bf), pltpu.VMEM((2 * C, D), bf), pltpu.VMEM((2 * C, ff), bf),
            dma((6,)), dma((2, 2)), dma((2, q)), dma((2, 2)), dma((2, q)),
            dma((2, n)), dma((2, n)), dma((2, n)), dma((2, n)), dma((2, n))],
        compiler_params=pltpu.CompilerParams(collective_id=cid, has_side_effects=True, vmem_limit_bytes=67043328),
        cost_estimate=pl.CostEstimate(flops=2 * t * D * (ka + 3 * ff), bytes_accessed=60_000_000, transcendentals=t * ff),
        name=f"ffn{layer}",
    )(a, h, gains, w_o, w_gate, w_up, w_down)


LOCAL_BASE = 10000.0
GLOBAL_BASE = 1000000.0
def tables(pos, base):
    half = 64
    inv_freq = base ** (-jnp.arange(half, dtype=jnp.float32) / half)
    angles = pos.astype(jnp.float32)[:, None] * inv_freq
    c, s = jnp.cos(angles), jnp.sin(angles)
    return jnp.concatenate([c, c], axis=1), jnp.concatenate([-s, s], axis=1)
def solution(mesh):
    def device_fn(x, pos, gains, w_q, w_k, w_v, w_o, w_gate, w_up, w_down):
        h = x
        outs = []
        wo = w_o.reshape(2, 1024, 2560)
        for l in (0, 1):
            local = l == 0
            cos, sin = tables(pos, LOCAL_BASE if local else GLOBAL_BASE)
            wkv = jnp.concatenate([w_k[l].reshape(2560, 256), w_v[l].reshape(2560, 256)], axis=1)
            wq = w_q[l].reshape(2560, 1024)
            a, kc, vc = attn(local, h, gains[l], cos, sin, wkv, wq, cid=l)
            outs += [kc[:, None, :], vc[:, None, :]]
            h = ffn(l, a, h, gains[l], wo, w_gate, w_up, w_down, cid=2 + l)
        return (h, *outs)
    token_spec = P(('rep', 'sp'), None)
    cache_spec = P('rep', ('tp', 'sp'), None)
    in_specs = (token_spec, P(('rep', 'sp')), P(), P(None, None, 'tp', None), P(None, None, 'tp', None),
                P(None, None, 'tp', None), P(None, 'tp', None, None), P(None, None, 'tp'), P(None, None, 'tp'),
                P(None, 'tp', None))
    out_specs = (token_spec, cache_spec, cache_spec, cache_spec, cache_spec)
    return jax.shard_map(device_fn, mesh=mesh, in_specs=in_specs, out_specs=out_specs, check_vma=False)
```

time: 2130 us -> 932 us (0.44)
  the two profiles are of different devices: /device:TPU:0 before, /device:TPU:5 now
where the time goes in v1:
time: 932 us
  Pallas kernels  896 us (96%)
  local copies, waits for them, and re-layouts  24.6 us (3%)
  other arithmetic  10.6 us (1%)
    pallas_call x2, Pallas kernels, ffn(): pl.pallas_call(functools.partial(ffn_kernel, layer, C), out_shape=jax.Sha...  754 us
    pallas_call x2, Pallas kernels, attn(): pl.pallas_call(functools.partial(attn_kernel, local), out_shape=[jax.Shap...  142 us

profile of v1, /device:TPU:5, one launch (start us, length us, event | category | flops | bytes accessed | tf_op | source)
XLA Modules:
  0.0 932.0 jit_solution(8382865145965496715)
XLA Ops:
  0.7 0.7 convert_element_type.4
  1.4 1.4 slice_bitcast_fusion
  2.8 0.0 copy-start
  2.8 3.7 fusion.5
  6.5 0.0 copy-done
  6.5 1.9 fusion.6
  8.3 0.5 copy_bitcast_fusion.4
  8.9 0.0 slice-start
  8.9 1.7 pad_maximum_fusion.wkv_hbm
  10.6 0.0 slice-start.1
  10.6 0.4 copy_bitcast_fusion.2
  11.0 1.8 pad_maximum_fusion.1.wkv_hbm
  12.8 0.0 slice-start.2
  12.8 3.7 fusion.1
  16.5 1.3 pad_maximum_fusion.4
  17.8 1.3 pad_maximum_fusion.2
  19.1 0.0 slice-done
  19.1 0.0 slice-done.1
  19.1 0.0 slice-done.2
  19.2 0.8 fusion.4
  19.9 3.7 copy.27
  23.6 3.7 copy.28
  27.3 36.6 %attn_local.1 = (bf16[1024,1024]{1,0:T(8,128)(2,1)}, bf16[512,128]{1,0:T(8,128)(2,1)}, bf16[512,128]{1,0:T(8,128)(2,1)}) custom-call(bf16[1024,2560]{1,0:T(8,128)(2,1)} %h_hbm.1, f32[4,2560]{1,0:T(4,128)} %get-tuple-element.24.g_ref, f32[1024,128]{1,0:T(8,128)} %get-tuple-element.34.cos_ref, f32[1024,128]{1,0:T(8,128)} %get-tuple-element.35.sin_ref, ...), custom_call_target="tpu_custom_call" | custom-call | flops 20000000000 | bytes 20000000 | tf_op jit(solution)/shard_map/attn_local/pallas_call | solution.py:270
  64.0 376.9 %ffn0.1.x_hbm.h_hbm = bf16[1024,2560]{1,0:T(8,128)(2,1)} custom-call(bf16[1024,1024]{1,0:T(8,128)(2,1)} %get-tuple-element.11.a_hbm, bf16[1024,2560]{1,0:T(8,128)(2,1)} %h_hbm.1, f32[4,2560]{1,0:T(4,128)} %get-tuple-element.24.g_ref, bf16[2,1024,2560]{2,1,0:T(8,128)(2,1)} %bitcast.49, bf16[2,2560,2432]{2,1,0:T(8,128)(2,1)} %wg_hbm.3, ...), custom_call_target="tpu_custom_call" | custom-call | flops 43620761600 | bytes 60000000 | tf_op jit(solution)/shard_map/ffn0/pallas_call | solution.py:486
  440.9 105.2 %attn_global.1 = (bf16[1024,1024]{1,0:T(8,128)(2,1)}, bf16[4096,128]{1,0:T(8,128)(2,1)}, bf16[4096,128]{1,0:T(8,128)(2,1)}) custom-call(bf16[1024,2560]{1,0:T(8,128)(2,1)} %ffn0.1.x_hbm.h_hbm, f32[4,2560]{1,0:T(4,128)} %get-tuple-element.23.g_ref, f32[1024,128]{1,0:T(8,128)} %get-tuple-element.36.cos_ref, f32[1024,128]{1,0:T(8,128)} %get-tuple-element.37.sin_ref, ...), custom_call_target="tpu_custom_call" | custom-call | flops 20000000000 | bytes 20000000 | tf_op jit(solution)/shard_map/attn_global/pallas_call | solution.py:270
  546.1 377.3 %ffn1.1 = bf16[1024,2560]{1,0:T(8,128)(2,1)} custom-call(bf16[1024,1024]{1,0:T(8,128)(2,1)} %get-tuple-element.12.a_hbm, bf16[1024,2560]{1,0:T(8,128)(2,1)} %ffn0.1.x_hbm.h_hbm, f32[4,2560]{1,0:T(4,128)} %get-tuple-element.23.g_ref, bf16[2,1024,2560]{2,1,0:T(8,128)(2,1)} %bitcast.50, bf16[2,2560,2432]{2,1,0:T(8,128)(2,1)} %wg_hbm.3, ...), custom_call_target="tpu_custom_call" | custom-call | flops 43620761600 | bytes 60000000 | tf_op jit(solution)/shard_map/ffn1/pallas_call | solution.py:486
  923.4 0.0 copy-start.4
  923.4 0.0 copy-start.3
  923.5 0.0 copy-start.2
  923.5 5.3 copy.34
  928.8 0.0 copy-done.4
  928.8 0.0 copy-start.1
  928.8 0.7 copy.35
  929.4 0.0 copy-done.3
  929.4 0.7 copy.36
  930.1 0.0 copy-done.2
  930.1 1.0 copy.37
  931.0 0.0 copy-done.1
  931.0 1.0 copy.38
  (3 shorter events, 0.0 us)
Async XLA Ops:
  2.8 3.7 copy-start
  8.9 10.3 %slice-start = ((s8[10485760]{0:T(1024)(128)(4,1)}), s8[4194304]{0:T(1024)(128)(4,1)S(1)}, s32[]{:S(2)}) async-start(s8[10485760]{0:T(1024)(128)(4,1)} %bitcast.37), calls=%async_computation | async-start | bytes 8388608
  10.6 8.6 slice-start.1
  12.8 6.4 slice-start.2
  923.4 5.3 copy-start.4
  923.4 6.0 copy-start.3
  923.5 6.6 copy-start.2
  928.8 2.3 copy-start.1

commit v2 on v0

v2 whole, which is shorter than its diff:
```python
import functools
import jax, jax.numpy as jnp
from jax import lax
from jax.experimental import pallas as pl
from jax.experimental.pallas import tpu as pltpu
from jax.sharding import PartitionSpec as P
MESH = pl.DeviceIdType.MESH
NORM_EPS = 1e-6
D = 2560
WINDOW = 512
HEAD = 128
CHUNK = 32
RING = 4
WD_KEPT = (6, 4)
WD_SLOTS = 2
SPAN = WINDOW + 128
KEYS = 512
LOG2E = 1.4426950408889634
LOCAL_BASE = 10000.0
GLOBAL_BASE = 1000000.0
NT = (((1,), (1,)), ((), ()))
BF, F32 = jnp.bfloat16, jnp.float32


def rms(v, gain):
    return v * lax.rsqrt(jnp.mean(v * v, axis=-1, keepdims=True) + NORM_EPS) * gain


def at(start, size):
    return pl.ds(pl.multiple_of(start, size), size)


def layer_kernel(layer, *refs):
    it = iter(refs)

    def take(k):
        return [next(it) for _ in range(k)]

    if layer == 0:
        x_hbm, g_ref, tab_hbm, wq_hbm, wkv_hbm = take(5)
    else:
        res_hbm, q_hbm, kv_hbm, g_ref = take(4)
    wo_hbm, wg_hbm, wu_hbm, wd_hbm = take(4)
    if layer == 0:
        out_hbm, q1_hbm, kv1_hbm, kc_hbm, vc_hbm = take(5)
    else:
        out_hbm, kc_hbm, vc_hbm = take(3)
    wa, wg_v, wu_v, wd_v, wd_b, q_v, kv, hb, ub, so, sm, ro, rm, lhs_a, lhs_u, fb = take(16)
    w_sem, wo_sem, wk_sem, wd_sem, os_sem, or_sem, ms_sem, mr_sem, us_sem, ur_sem, hs_sem, hr_sem, out_sem, c_sem = take(14)
    if layer == 0:
        tab, wkv_v, uq, qs, ks, cache = take(6)
        (wq_sem, wkv_sem, halo_s, halo_r, tail_s, tail_r, pair_s, pair_r, far_s, far_r, own_s, fwd_s, fwd_r, q_sem) = take(14)
    else:
        st, sc_v = take(2)

    z = lax.axis_index('tp')
    s = lax.axis_index('sp')
    C = CHUNK
    n = hb.shape[0]
    half = n * C
    rows = 2 * half
    ff = wg_v.shape[1]
    scale = HEAD ** -0.5 * LOG2E
    r = (z, 3 - z)
    down = {'tp': jnp.maximum(z - 1, 0)}
    up = {'tp': jnp.minimum(z + 1, 3)}
    toward, away = (down, up), (up, down)
    is_end = (z == 0) | (z == 3)
    pair = {'sp': s + 1 - 2 * lax.rem(s, 2)}
    far_id = lax.rem(s + 2, 4)
    far = {'sp': far_id}

    def load(k, src, dst):
        return pltpu.make_async_copy(src, dst, w_sem.at[k])

    wo_tiles = [pltpu.make_async_copy(wo_hbm.at[layer, :, pl.ds(j * 256, 256)], wa.at[pl.ds(j * 1024, 1024), :], wo_sem.at[j])
                for j in range(D // 256)]
    wg_load = load(0, wg_hbm.at[layer], wg_v)
    wu_load = load(1, wu_hbm.at[layer], wu_v)
    res_half = jnp.where(z == 3, 1, 0)
    if layer == 0:
        res_load = load(2, x_hbm.at[res_half], hb)
        def wkv_loads(l):
            return [pltpu.make_async_copy(wkv_hbm.at[l, h], wkv_v.at[:, pl.ds(h * HEAD, HEAD)], wkv_sem.at[h]) for h in range(4)]
        wq_first = [pltpu.make_async_copy(wq_hbm.at[0, h], wu_v.at[:, pl.ds(h * HEAD, HEAD)], wq_sem.at[h]) for h in range(8)]
        first = [load(3, x_hbm, ub), load(4, tab_hbm.at[0], tab)] + wkv_loads(0) + wq_first
    else:
        res_load = load(2, res_hbm, hb)
        first = [load(3, q_hbm, q_v), load(4, kv_hbm, kv)]
    for c in first:
        c.start()
    for c in wo_tiles:
        c.start()

    @pl.when(is_end)
    def _():
        res_load.start()
    wg_load.start()
    if layer == 1:
        wu_load.start()

    bar = pltpu.get_barrier_semaphore()

    @pl.when(z > 0)
    def _():
        pl.semaphore_signal(bar, inc=1, device_id=down, device_id_type=MESH)

    @pl.when(z < 3)
    def _():
        pl.semaphore_signal(bar, inc=1, device_id=up, device_id_type=MESH)
    if layer == 0:
        for k in (1, 2, 3):
            pl.semaphore_signal(bar, inc=1, device_id={'sp': lax.rem(s + k, 4)}, device_id_type=MESH)
    pl.semaphore_wait(bar, jnp.where(is_end, 1, 2) + (3 if layer == 0 else 0))

    kept = WD_KEPT[layer]
    flow = D // 256 - kept

    def wd_tile(k):
        slot = lax.rem(k, WD_SLOTS)
        return pltpu.make_async_copy(wd_hbm.at[layer, :, at((kept + lax.rem(k, flow)) * 256, 256)], wd_b.at[slot], wd_sem.at[slot])
    wd_total = (n + 3) * flow
    wd_loads = [pltpu.make_async_copy(wd_hbm.at[layer, :, pl.ds(j * 256, 256)], wd_v.at[j], wk_sem.at[j]) for j in range(kept)]

    def rotor(cs):
        low = lax.broadcasted_iota(jnp.int32, cs.shape, 1) < HEAD // 2
        other = pltpu.roll(cs, HEAD // 2, 1)
        cos, sin = jnp.where(low, cs, other), jnp.where(low, -other, cs)
        return lambda v: v * cos + pltpu.roll(v, HEAD // 2, 1) * sin

    if layer == 0:
        kv[:, pl.ds(WINDOW + rows, SPAN - WINDOW), :] = jnp.zeros((4, SPAN - WINDOW, HEAD), BF)

        @pl.when(s == 0)
        def _():
            kv[:, :WINDOW, :] = jnp.zeros((4, WINDOW, HEAD), BF)

        halo = pltpu.make_async_remote_copy(kv.at[:, pl.ds(rows, WINDOW), :], kv.at[:, pl.ds(0, WINDOW), :],
                                            halo_s, halo_r, device_id={'sp': jnp.minimum(s + 1, 3)}, device_id_type=MESH)

        def tail(dst, kind):
            return pltpu.make_async_remote_copy(kv.at[2 * kind + dst // 2, pl.ds(rows, WINDOW), :], cache.at[kind],
                                                tail_s.at[dst, kind], tail_r.at[kind], device_id={'sp': dst}, device_id_type=MESH)
        B = 256
        per = B // C
        blocks = half // B
        for c in first[:6]:
            c.wait()

        def kv_block(k, _):
            d = 1 - k // blocks
            i0 = lax.rem(k, blocks) * per
            row = d * half + i0 * C

            def norm(i, _):
                ub[d, i0 + i] = rms(ub[d, i0 + i].astype(F32), g_ref[0, 0:1, :]).astype(BF)
                return 0
            lax.fori_loop(0, per, norm, 0, unroll=2)
            p = jnp.dot(ub[d, at(i0, per)].reshape(B, D), wkv_v[...], preferred_element_type=F32)
            rope = rotor(tab[at(row, B), :])
            dst = at(WINDOW + row, B)
            for h in range(2):
                kv[h, dst, :] = rope(p[:, h * HEAD:(h + 1) * HEAD]).astype(BF)
                kv[2 + h, dst, :] = p[:, (2 + h) * HEAD:(3 + h) * HEAD].astype(BF)

            @pl.when(k == blocks - 1)
            def _():
                @pl.when(s < 3)
                def _():
                    halo.start()

                @pl.when(s == 3)
                def _():
                    for dst in range(3):
                        for kind in range(2):
                            tail(dst, kind).start()
            return 0
        lax.fori_loop(0, 2 * blocks, kv_block, 0)
        for c in wkv_loads(1):
            c.start()
        for c in wq_first:
            c.wait()

        def q_block(k, _):
            d = k // blocks
            i0 = lax.rem(k, blocks) * per
            rope = rotor(tab[at(d * half + i0 * C, B), :])
            u = ub[d, at(i0, per)].reshape(B, D)
            for c in range(4):
                p = jnp.dot(u, wu_v[:, c * 256:(c + 1) * 256], preferred_element_type=F32)
                for e in range(2):
                    qe = rope(p[:, e * HEAD:(e + 1) * HEAD]).astype(BF)
                    h = (c % 2) * 2 + e
                    for i in range(per):
                        q_v[d, i0 + i, c // 2, h * C:(h + 1) * C, :] = qe[i * C:(i + 1) * C]
            return 0
        lax.fori_loop(0, 2 * blocks, q_block, 0)
        wu_load.start()
        load(4, tab_hbm.at[1], tab).start()

    @pl.when(is_end)
    def _():
        res_load.wait()
    for c in wd_loads:
        c.start()
    for k in range(WD_SLOTS):
        wd_tile(k).start()

    def place(d, g, o):
        for h in range(4):
            lhs_a[d * C:(d + 1) * C, (g * 4 + h) * HEAD:(g * 4 + h + 1) * HEAD] = o[h * C:(h + 1) * C].astype(BF)

    def chunk_at(t, d):
        return jnp.clip(t - 3 + r[d], 0, n - 1)

    def row_col(shape):
        return (lax.rem(lax.broadcasted_iota(jnp.int32, shape, 0), C), lax.broadcasted_iota(jnp.int32, shape, 1))

    def attend_local(t):
        for d in range(2):
            i = chunk_at(t, d)
            keys = pl.ds(pl.multiple_of(d * half + i * C, C), SPAN)
            low = jnp.where(s == 0, WINDOW - d * half - i * C, 0)
            for g in range(2):
                sc = lax.dot_general(q_v[d, i, g], kv[g, keys, :], NT, preferred_element_type=F32) * scale
                row, col = row_col(sc.shape)
                sc = jnp.where((col > row) & (col <= row + WINDOW) & (col >= low), sc, -1e30)
                p = jnp.exp2(sc - jnp.max(sc, axis=1, keepdims=True))
                o = jnp.dot(p.astype(BF), kv[2 + g, keys, :], preferred_element_type=F32)
                place(d, g, o / jnp.sum(p, axis=1, keepdims=True))

    def attend_global(t):
        ids = [chunk_at(t, d) for d in range(2)]
        streams = [(d, g) for d in range(2) for g in range(2)]
        for d, g in streams:
            st[d, g, 0] = jnp.full((4 * C, HEAD), -1e30, F32)
            st[d, g, 1] = jnp.zeros((4 * C, HEAD), F32)
            st[d, g, 2] = jnp.zeros((4 * C, HEAD), F32)

        def score(slot, d, g, b):
            sc_v[slot, d, g] = lax.dot_general(q_v[d, ids[d], g], kv[g, at(b * KEYS, KEYS), :], NT, preferred_element_type=F32)

        def update(slot, d, g, b, masked=False):
            sc = sc_v[slot, d, g]
            if masked:
                row, col = row_col(sc.shape)
                sc = jnp.where(col <= row + ids[d] * C, sc, -1e30)
            old = st[d, g, 0]
            new = jnp.maximum(old, jnp.max(sc, axis=1, keepdims=True))
            alpha = jnp.exp2((old - new) * scale)
            parts = [jnp.exp2((sc[:, c * HEAD:(c + 1) * HEAD] - new) * scale) for c in range(KEYS // HEAD)]
            st[d, g, 1] = st[d, g, 1] * alpha + sum(parts[1:], parts[0])
            p = jnp.concatenate(parts, axis=1).astype(BF)
            st[d, g, 2] = st[d, g, 2] * alpha + jnp.dot(p, kv[2 + g, at(b * KEYS, KEYS), :], preferred_element_type=F32)
            st[d, g, 0] = new

        for d, g in streams:
            score(0, d, g, 0)

        def two(j, _):
            for e in range(2):
                for d, g in streams:
                    score(1 - e, d, g, 2 * j + e + 1)
                for d, g in streams:
                    update(e, d, g, 2 * j + e)
            return 0
        lax.fori_loop(0, s, two, 0)
        for g in range(2):
            score(1, 1, g, 2 * s + 1)
        for d, g in streams:
            update(0, d, g, 2 * s, masked=d == 0)
        for g in range(2):
            update(1, 1, g, 2 * s + 1, masked=True)
        for d, g in streams:
            place(d, g, st[d, g, 2] / jnp.sum(st[d, g, 1], axis=1, keepdims=True))

    if layer == 0:
        @pl.when(s > 0)
        def _():
            halo.wait_recv()
        attend = attend_local
    else:
        for c in first:
            c.wait()
        y = s // 2
        caches = [pltpu.make_async_copy(kv.at[y], kc_hbm, c_sem.at[0]), pltpu.make_async_copy(kv.at[2 + y], vc_hbm, c_sem.at[1])]
        for c in caches:
            c.start()
        attend = attend_global
    attend(0)
    for c in wo_tiles:
        c.wait()

    def red_copy(stage, recv, s_sem, r_sem, d, slot, i):
        k = lax.rem(i, RING)
        return pltpu.make_async_remote_copy(stage.at[slot, d], recv.at[d, k], s_sem.at[slot, d], r_sem.at[d, k],
                                            device_id=toward[d], device_id_type=MESH)

    def cast_copy(s_sem, r_sem, d, i):
        return pltpu.make_async_remote_copy(ub.at[d, i], ub.at[d, i], s_sem.at[d, i], r_sem.at[d, i],
                                            device_id=away[d], device_id_type=MESH)

    def out_copy(d, i):
        return pltpu.make_async_copy(ub.at[d, i], out_hbm.at[i] if layer == 0 else out_hbm.at[d, i], out_sem.at[d, i])

    if layer == 0:
        wq_tiles = [pltpu.make_async_copy(wq_hbm.at[1, h], wa.at[pl.ds(h // 2 * D, D), pl.ds(h % 2 * HEAD, HEAD)], wq_sem.at[h]) for h in range(8)]
        pairs = n // 2

        def span_of(dev, d, k):
            return kv1_hbm.at[:, at(dev * rows + d * half + k * 2 * C, 2 * C), :]

        def kv_own(d, k):
            slot = lax.rem(k, 2)
            return pltpu.make_async_copy(ks.at[slot, d], span_of(s, d, k), own_s.at[slot, d])

        def kv_pair(d, k):
            slot = lax.rem(k, 2)
            return pltpu.make_async_remote_copy(ks.at[slot, d], span_of(s, d, k), pair_s.at[slot, d], pair_r.at[d, k],
                                                device_id=pair, device_id_type=MESH)

        def kv_far(d, k):
            slot = lax.rem(k, 2)
            return pltpu.make_async_remote_copy(ks.at[slot, d], span_of(s, d, k), far_s.at[slot, d], far_r.at[d, k],
                                                device_id=far, device_id_type=MESH)

        def kv_fwd(d, k):
            ref = span_of(far_id, d, k)
            return pltpu.make_async_remote_copy(ref, ref, fwd_s.at[d, k], fwd_r.at[d, k], device_id=pair, device_id_type=MESH)

        def q_out(d, k):
            slot = lax.rem(k, 2)
            return pltpu.make_async_copy(qs.at[slot, d], q1_hbm.at[d, at(2 * k, 2)], q_sem.at[slot, d])

        def sent(k):
            for d in range(2):
                kv_own(d, k).wait()
                kv_pair(d, k).wait_send()
                kv_far(d, k).wait_send()
                q_out(d, k).wait()

        def forward(k):
            for d in range(2):
                kv_far(d, k).wait_recv()
                kv_fwd(d, k).start()

        def next_qkv(k):
            slot = lax.rem(k, 2)

            @pl.when(k >= 2)
            def _():
                sent(k - 2)
            M = 2 * C
            for d in range(2):
                uq[d * M:(d + 1) * M, :] = rms(ub[d, at(2 * k, 2)].reshape(M, D).astype(F32), g_ref[1, 0:1, :]).astype(BF)
            ropes = [rotor(tab[at(d * half + k * M, M), :]) for d in range(2)]
            p = jnp.dot(uq[...], wkv_v[...], preferred_element_type=F32)
            for d in range(2):
                for h in range(2):
                    ks[slot, d, h] = ropes[d](p[d * M:(d + 1) * M, h * HEAD:(h + 1) * HEAD]).astype(BF)
                    ks[slot, d, 2 + h] = p[d * M:(d + 1) * M, (2 + h) * HEAD:(3 + h) * HEAD].astype(BF)
                kv_own(d, k).start()
                kv_pair(d, k).start()
                kv_far(d, k).start()
            for c in range(4):
                p = jnp.dot(uq[...], wa[c * D:(c + 1) * D, :], preferred_element_type=F32)
                for d in range(2):
                    for e in range(2):
                        qe = ropes[d](p[d * M:(d + 1) * M, e * HEAD:(e + 1) * HEAD]).astype(BF)
                        h = (c % 2) * 2 + e
                        for i in range(2):
                            qs[slot, d, i, c // 2, h * C:(h + 1) * C, :] = qe[i * C:(i + 1) * C]
            for d in range(2):
                q_out(d, k).start()

            @pl.when(k >= 1)
            def _():
                forward(k - 1)

    def tick(t, _):
        slot = lax.rem(t, 2)

        def free_stage(stage, recv, s_sem, r_sem, first_tick):
            for d in (0, 1):
                i = t - first_tick - 3 + r[d] - 2

                @pl.when((i >= 0) & (i < n) & (r[d] > 0))
                def _():
                    red_copy(stage, recv, s_sem, r_sem, d, slot, i).wait_send()

        def reduce(stage, recv, s_sem, r_sem, first_tick, at_end):
            for d in (0, 1):
                i = t - first_tick - 3 + r[d]
                act = (i >= 0) & (i < n)

                @pl.when(act & (r[d] < 3))
                def _():
                    red_copy(stage, recv, s_sem, r_sem, d, slot, i).wait_recv()
                    stage[slot, d] += recv[d, lax.rem(i, RING)]

                @pl.when(act & (r[d] > 0))
                def _():
                    red_copy(stage, recv, s_sem, r_sem, d, slot, i).start()

                @pl.when(act & (r[d] == 0))
                def _():
                    at_end(d, i)

        def spread(s_sem, r_sem, first_tick, then):
            for d in (0, 1):
                i = t - first_tick - r[d]
                act = (i >= 0) & (i < n) & (r[d] > 0)

                @pl.when(act)
                def _():
                    cast_copy(s_sem, r_sem, d, i).wait_recv()

                @pl.when(act & (r[d] < 3))
                def _():
                    cast_copy(s_sem, r_sem, d, i).start()
                if then is not None:
                    @pl.when(act)
                    def _():
                        then(d, i)

        free_stage(so, ro, os_sem, or_sem, 0)

        @pl.when(t < n + 3)
        def _():
            def cols(j, _):
                cs = at(j * 256, 256)
                p = jnp.dot(lhs_a[...], wa[at(j * 1024, 1024), :], preferred_element_type=F32)
                so[slot, 0, :, cs] = p[:C]
                so[slot, 1, :, cs] = p[C:]
                return 0
            lax.fori_loop(0, D // 256, cols, 0, unroll=5)

        def o_end(d, i):
            h1 = (hb[i].astype(F32) + rms(so[slot, d], g_ref[layer, 1:2, :])).astype(BF)
            hb[i] = h1
            ub[d, i] = rms(h1.astype(F32), g_ref[layer, 2:3, :]).astype(BF)
            cast_copy(us_sem, ur_sem, d, i).start()
        reduce(so, ro, os_sem, or_sem, 0, o_end)
        spread(us_sem, ur_sem, 3, None)

        @pl.when(t + 1 < n + 3)
        def _():
            attend(t + 1)

        @pl.when(t == 6)
        def _():
            for c in [wg_load, wu_load] + wd_loads:
                c.wait()
        free_stage(sm, rm, ms_sem, mr_sem, 6)

        @pl.when((t >= 6) & (t < n + 9))
        def _():
            for d in (0, 1):
                i = t - 9 + r[d]

                @pl.when((i >= 0) & (i < n) & (r[d] < 3))
                def _():
                    cast_copy(us_sem, ur_sem, d, i).wait_send()

                @pl.when((i >= 0) & (i < n))
                def _():
                    lhs_u[pl.ds(d * C, C), :] = ub[d, jnp.clip(i, 0, n - 1)]

            def hidden(cs):
                gate = jnp.dot(lhs_u[...], wg_v[:, cs], preferred_element_type=F32)
                upper = jnp.dot(lhs_u[...], wu_v[:, cs], preferred_element_type=F32)
                fb[:, cs] = (gate / (1.0 + jnp.exp(-gate)) * upper).astype(BF)

            def hcols(j, _):
                hidden(at(j * 256, 256))
                return 0
            lax.fori_loop(0, ff // 256, hcols, 0, unroll=3)
            if ff % 256:
                hidden(pl.ds(ff // 256 * 256, ff % 256))

            def down_tile(w, j):
                cs = pl.ds(j * 256, 256)
                p = jnp.dot(fb[...], w, preferred_element_type=F32)
                sm[slot, 0, :, cs] = p[:C]
                sm[slot, 1, :, cs] = p[C:]

            def flowing(j):
                k = (t - 6) * flow + j
                wd_tile(k).wait()
                down_tile(wd_b[lax.rem(k, WD_SLOTS)], kept + j)

                @pl.when(k + WD_SLOTS < wd_total)
                def _():
                    wd_tile(k + WD_SLOTS).start()
            for j in range(max(kept, flow)):
                if j < flow:
                    flowing(j)
                if j < kept:
                    down_tile(wd_v[j], j)

        def m_end(d, i):
            ub[d, i] = (hb[i].astype(F32) + rms(sm[slot, d], g_ref[layer, 3:4, :])).astype(BF)
            cast_copy(hs_sem, hr_sem, d, i).start()
            out_copy(d, i).start()
        reduce(sm, rm, ms_sem, mr_sem, 6, m_end)
        spread(hs_sem, hr_sem, 9, None if layer == 0 else lambda d, i: out_copy(d, i).start())

        if layer == 0:
            @pl.when(t == n + 3)
            def _():
                for c in wq_tiles:
                    c.start()
            first_qkv = n + 12 - pairs

            @pl.when(t == first_qkv)
            def _():
                for c in wkv_loads(1) + [load(4, tab_hbm.at[1], tab)] + wq_tiles:
                    c.wait()

            @pl.when(t >= first_qkv)
            def _():
                next_qkv(t - first_qkv)
        return 0

    lax.fori_loop(0, n + 12, tick, 0)

    if layer == 0:
        forward(pairs - 1)

        @pl.when(s < 3)
        def _():
            halo.wait_send()
            for kind in range(2):
                tail(0, kind).wait_recv()

        @pl.when(s == 3)
        def _():
            for dst in range(3):
                for kind in range(2):
                    tail(dst, kind).wait_send()
            for kind in range(2):
                cache[kind] = kv[2 * kind + 1, pl.ds(rows, WINDOW), :]
        caches = [pltpu.make_async_copy(cache.at[0], kc_hbm, c_sem.at[0]), pltpu.make_async_copy(cache.at[1], vc_hbm, c_sem.at[1])]
        for c in caches:
            c.start()
        for k in (pairs - 2, pairs - 1):
            sent(k)

        def got(k, _):
            for d in range(2):
                kv_pair(d, k).wait_recv()
                kv_fwd(d, k).wait()
            return 0
        lax.fori_loop(0, pairs, got, 0)

    def drain(i, _):
        for d in (0, 1):
            @pl.when(r[d] < 3)
            def _():
                cast_copy(hs_sem, hr_sem, d, i).wait_send()
            if layer == 0:
                @pl.when(r[d] == 0)
                def _():
                    out_copy(d, i).wait()
            else:
                out_copy(d, i).wait()
        return 0
    lax.fori_loop(0, n, drain, 0)
    for c in caches:
        c.wait()


def run_layer(layer, heads, weights, out_shape):
    dma = pltpu.SemaphoreType.DMA
    any_, vmem = pl.BlockSpec(memory_space=pl.ANY), pl.BlockSpec(memory_space=pltpu.VMEM)
    ka, ff = weights[0].shape[1], weights[1].shape[2]
    C = CHUNK
    n = out_shape[0].shape[-3]
    rows = 2 * n * C
    keys = WINDOW + rows + SPAN - WINDOW if layer == 0 else 4 * rows
    scratch = [
        pltpu.VMEM((ka * D // 256, 256), BF), pltpu.VMEM((D, ff), BF), pltpu.VMEM((D, ff), BF), pltpu.VMEM((WD_KEPT[layer], ff, 256), BF), pltpu.VMEM((WD_SLOTS, ff, 256), BF),
        pltpu.VMEM((2, n, 2, 4 * C, HEAD), BF), pltpu.VMEM((4, keys, HEAD), BF),
        pltpu.VMEM((n, C, D), BF), pltpu.VMEM((2, n, C, D), BF),
        pltpu.VMEM((2, 2, C, D), F32), pltpu.VMEM((2, 2, C, D), F32),
        pltpu.VMEM((2, RING, C, D), F32), pltpu.VMEM((2, RING, C, D), F32),
        pltpu.VMEM((2 * C, ka), BF), pltpu.VMEM((2 * C, D), BF), pltpu.VMEM((2 * C, ff), BF),
        dma((7,)), dma((D // 256,)), dma((WD_KEPT[layer],)), dma((WD_SLOTS,)), dma((2, 2)), dma((2, RING)), dma((2, 2)), dma((2, RING)),
        dma((2, n)), dma((2, n)), dma((2, n)), dma((2, n)), dma((2, n)), dma((2,))]
    if layer == 0:
        p = n // 2
        scratch += [
            pltpu.VMEM((rows, HEAD), F32), pltpu.VMEM((D, 4 * HEAD), BF), pltpu.VMEM((4 * C, D), BF),
            pltpu.VMEM((2, 2, 2, 2, 4 * C, HEAD), BF), pltpu.VMEM((2, 2, 4, 2 * C, HEAD), BF), pltpu.VMEM((2, WINDOW, HEAD), BF),
            dma((8,)), dma((4,)), dma, dma, dma((3, 2)), dma((2,)), dma((2, 2)), dma((2, p)), dma((2, 2)), dma((2, p)), dma((2, 2)),
            dma((2, p)), dma((2, p)), dma((2, 2))]
        in_specs = [any_, vmem] + [any_] * 3
    else:
        scratch += [pltpu.VMEM((2, 2, 3, 4 * C, HEAD), F32), pltpu.VMEM((2, 2, 2, 4 * C, KEYS), F32)]
        in_specs = [any_, any_, any_, vmem]
    return pl.pallas_call(
        functools.partial(layer_kernel, layer),
        out_shape=out_shape,
        in_specs=in_specs + [any_] * 4,
        out_specs=[any_] * len(out_shape),
        scratch_shapes=scratch,
        compiler_params=pltpu.CompilerParams(collective_id=layer, has_side_effects=True, vmem_limit_bytes=67043328),
        cost_estimate=pl.CostEstimate(flops=2 * rows * D * (ka + 3 * ff), bytes_accessed=300_000_000, transcendentals=rows * ff),
        name=f'layer{layer}',
    )(*heads, *weights)


def solution(mesh):
    def device_fn(x, pos, gains, w_q, w_k, w_v, w_o, w_gate, w_up, w_down):
        C = CHUNK
        rows = x.shape[0]
        n = rows // 2 // C
        shape = jax.ShapeDtypeStruct
        heads_first = (0, 2, 1, 3)
        wq = jnp.transpose(w_q, heads_first)
        wkv = jnp.concatenate([jnp.transpose(w_k, heads_first), jnp.transpose(w_v, heads_first)], axis=1)
        half = HEAD // 2
        freq = jnp.stack([base ** (-jnp.arange(half, dtype=F32) / half) for base in (LOCAL_BASE, GLOBAL_BASE)])
        angles = pos.astype(F32)[None, :, None] * freq[:, None, :]
        tab = jnp.concatenate([jnp.cos(angles), jnp.sin(angles)], axis=2)
        weights = (w_o.reshape(2, 8 * HEAD, D), w_gate, w_up, w_down)
        qshape = shape((2, n, 2, 4 * C, HEAD), BF)
        res, q1, kv1, kl, vl = run_layer(
            0, (x.reshape(2, n, C, D), gains, tab, wq, wkv), weights,
            [shape((n, C, D), BF), qshape, shape((4, 4 * rows, HEAD), BF), shape((WINDOW, HEAD), BF), shape((WINDOW, HEAD), BF)])
        out, kg, vg = run_layer(
            1, (res, q1, kv1, gains), weights,
            [shape((2, n, C, D), BF), shape((4 * rows, HEAD), BF), shape((4 * rows, HEAD), BF)])
        return (out.reshape(rows, D), kl[:, None, :], vl[:, None, :], kg[:, None, :], vg[:, None, :])

    token_spec = P(('rep', 'sp'), None)
    cache_spec = P('rep', ('tp', 'sp'), None)
    in_specs = (token_spec, P(('rep', 'sp')), P(), P(None, None, 'tp', None), P(None, None, 'tp', None),
                P(None, None, 'tp', None), P(None, 'tp', None, None), P(None, None, 'tp'), P(None, None, 'tp'),
                P(None, 'tp', None))
    out_specs = (token_spec, cache_spec, cache_spec, cache_spec, cache_spec)
    return jax.shard_map(device_fn, mesh=mesh, in_specs=in_specs, out_specs=out_specs, check_vma=False)
```

time: 2130 us -> 837 us (0.39)
  waiting for transfers between devices: 1510 us -> 0 us
  Pallas kernels: 0 us -> 804 us
  matrix products: 305 us -> 0 us
  other arithmetic: 115 us -> 8.68 us
  local copies, waits for them, and re-layouts: 82.8 us -> 19.1 us
  blocking collectives: 56.5 us -> 0 us
  loops' own time: 22.2 us -> 0 us
  starting transfers between devices: 21.4 us -> 0 us
    psum x4 -> x0, waiting for transfers between devices: 1410 us -> none  [the longest x2 712 us: layer(): lax.psum(jnp.einsum('the,hed->td', attn_back, w_o, preferred_element_type...]
    pallas_call x0 -> x2, Pallas kernels: none -> 804 us  [run_layer(): pl.pallas_call(functools.partial(layer_kernel, layer), out_shape=out_shap...]
    dot_general x74 -> x0, matrix products: 276 us -> none  [the longest x32 72.7 us: one_block(): jnp.einsum('qhgd,khd->hgqk', q_tile, k_tile, preferred_element_type=jnp.f...]
    all_to_all x2 -> x0, waiting for transfers between devices: 96.4 us -> none  [layer(): received = lax.all_to_all(outgoing, 'sp', 1, 0, tiled=True)]
    reduce_sum x40 -> x0, other arithmetic: 76.9 us -> none  [the longest x8 52.9 us: rms_norm(): jnp.mean(wide * wide, axis=-1, keepdims=True) + NORM_EPS]
    all_to_all x2 -> x0, blocking collectives: 56.5 us -> none  [layer(): lax.all_to_all(attn_out, 'sp', 0, 2, tiled=True)]
    unnamed x4 -> x0, matrix products: 28.5 us -> none
    another operation x2 -> x0, loops' own time: 22.2 us -> none  [attend(): blocks = lax.map(one_block, jnp.arange(q_heads.shape[0] // Q_BLOCK))]
  transfers between devices with their start and end apart: 6 -> 0, of which waited for: 6 -> 0; matrix products, arithmetic and copies ran while one was open for 1% -> 0% of each run, Pallas kernels for 0% -> 0%
where the time goes in v2:
time: 837 us; the launch traced here: 833 us
  Pallas kernels  804 us (96%)
  local copies, waits for them, and re-layouts  19.1 us (2%)
  other arithmetic  8.68 us (1%)
    pallas_call x2, Pallas kernels, run_layer(): pl.pallas_call(functools.partial(layer_kernel, layer), out_shape=out_shap...  804 us
    unnamed x18, local copies, waits for them, and re-layouts  18.4 us

profile of v2, /device:TPU:0, one launch (start us, length us, event | category | flops | bytes accessed | tf_op | source)
XLA Modules:
  0.0 832.8 jit_solution(17572259521525920241)
XLA Ops:
  0.6 0.0 copy-start
  0.6 0.0 copy-start.1
  0.7 0.8 convert_element_type.3
  1.5 3.7 multiply_cosine_fusion
  5.2 1.3 pad_maximum_fusion.1.refs_2_
  6.5 0.0 copy-done
  6.5 0.0 copy-done.1
  6.5 0.7 copy_bitcast_fusion.1
  7.2 2.8 pad_maximum_fusion.refs_4_
  10.0 9.8 %copy.21 = bf16[2,2560,8,128]{3,1,2,0:T(8,128)(2,1)} copy(bf16[2,2560,8,128]{3,2,1,0:T(8,128)(2,1)} %param.13) | data formatting | bytes 20971520 | tf_op args[3]
  19.8 410.6 %layer0.1 = (bf16[16,32,2560]{2,1,0:T(8,128)(2,1)}, bf16[2,16,2,128,128]{4,3,2,1,0:T(8,128)(2,1)}, bf16[4,4096,128]{2,1,0:T(8,128)(2,1)}, bf16[512,128]{1,0:T(8,128)(2,1)}, bf16[512,128]{1,0:T(8,128)(2,1)}) custom-call(bf16[2,16,32,2560]{3,2,1,0:T(8,128)(2,1)} %bitcast.22, f32[2,4,2560]{2,1,0:T(4,128)} %refs_3_.1, ...), custom_call_target="tpu_custom_call" | custom-call | flops 43620761600 | bytes 300000000 | tf_op jit(solution)/shard_map/layer0/pallas_call | solution.py:601
  430.5 393.7 %layer1.1 = (bf16[2,16,32,2560]{3,2,1,0:T(8,128)(2,1)}, bf16[4096,128]{1,0:T(8,128)(2,1)}, bf16[4096,128]{1,0:T(8,128)(2,1)}) custom-call(bf16[16,32,2560]{2,1,0:T(8,128)(2,1)} %get-tuple-element.13.refs_0_, bf16[2,16,2,128,128]{4,3,2,1,0:T(8,128)(2,1)} %get-tuple-element.14.refs_1_, bf16[4,4096,128]{2,1,0:T(8,128)(2,1)} %get-tuple-element.15.refs_2_, ...), custom_call_target="tpu_custom_call" | custom-call | flops 43620761600 | bytes 300000000 | tf_op jit(solution)/shard_map/layer1/pallas_call | solution.py:601
  824.2 0.0 copy-start.5
  824.2 0.0 copy-start.4
  824.2 0.0 copy-start.3
  824.2 0.0 copy-start.2
  824.2 5.3 copy.27
  829.6 0.0 copy-done.5
  829.6 0.7 copy.28
  830.2 0.0 copy-done.4
  830.2 0.7 copy.29
  830.9 0.0 copy-done.3
  830.9 1.0 copy.30
  831.8 0.0 copy-done.2
  831.8 1.0 copy.31
  (2 shorter events, 0.0 us)
Async XLA Ops:
  0.6 5.9 copy-start
  0.6 5.9 copy-start.1
  824.2 5.4 copy-start.5
  824.2 6.0 copy-start.4
  824.2 6.7 copy-start.3
  824.2 7.6 copy-start.2

commit v3 on v2

--- a/solution.py
+++ b/solution.py
@@ -11,7 +11,7 @@
 HEAD = 128
 CHUNK = 32
 RING = 4
-WD_KEPT = (6, 4)
+WD_KEPT = (4, 4)
 WD_SLOTS = 2
 SPAN = WINDOW + 128
 KEYS = 512
@@ -37,19 +37,20 @@
         return [next(it) for _ in range(k)]
 
     if layer == 0:
-        x_hbm, g_ref, tab_hbm, wq_hbm, wkv_hbm = take(5)
+        x_hbm, g_ref, tab_hbm, wq_hbm, wk_hbm, wv_hbm = take(6)
     else:
         res_hbm, q_hbm, kv_hbm, g_ref = take(4)
     wo_hbm, wg_hbm, wu_hbm, wd_hbm = take(4)
     if layer == 0:
-        out_hbm, q1_hbm, kv1_hbm, kc_hbm, vc_hbm = take(5)
+        out_hbm, q1_hbm, kv1_hbm, kc_hbm, vc_hbm, wq1_hbm, wkv1_hbm = take(7)
     else:
         out_hbm, kc_hbm, vc_hbm = take(3)
     wa, wg_v, wu_v, wd_v, wd_b, q_v, kv, hb, ub, so, sm, ro, rm, lhs_a, lhs_u, fb = take(16)
-    w_sem, wo_sem, wk_sem, wd_sem, os_sem, or_sem, ms_sem, mr_sem, us_sem, ur_sem, hs_sem, hr_sem, out_sem, c_sem = take(14)
-    if layer == 0:
-        tab, wkv_v, uq, qs, ks, cache = take(6)
-        (wq_sem, wkv_sem, halo_s, halo_r, tail_s, tail_r, pair_s, pair_r, far_s, far_r, own_s, fwd_s, fwd_r, q_sem) = take(14)
+    w_sem, wo_sem, wk_sem, wd_sem, os_sem, or_sem, ms_sem, mr_sem, us_sem, ur_sem, hs_sem, hr_sem, hx_sem, out_sem, c_sem = take(15)
+    if layer == 0:
+        tab, wkv_v, uq, qs, ks, cache, perm, qin, kvin, qo, kvo = take(11)
+        nat_sem, ri_sem, ro_sem = take(3)
+        (x_sem, wq_sem, wkv_sem, halo_s, halo_r, tail_s, tail_r, pair_s, pair_r, far_s, far_r, own_s, fwd_s, fwd_r, q_sem) = take(15)
     else:
         st, sc_v = take(2)
 
@@ -80,38 +81,38 @@
     res_half = jnp.where(z == 3, 1, 0)
     if layer == 0:
         res_load = load(2, x_hbm.at[res_half], hb)
-        def wkv_loads(l):
-            return [pltpu.make_async_copy(wkv_hbm.at[l, h], wkv_v.at[:, pl.ds(h * HEAD, HEAD)], wkv_sem.at[h]) for h in range(4)]
-        wq_first = [pltpu.make_async_copy(wq_hbm.at[0, h], wu_v.at[:, pl.ds(h * HEAD, HEAD)], wq_sem.at[h]) for h in range(8)]
-        first = [load(3, x_hbm, ub), load(4, tab_hbm.at[0], tab)] + wkv_loads(0) + wq_first
+        wkv_loads = [pltpu.make_async_copy(wkv1_hbm.at[h], wkv_v.at[:, pl.ds(h * HEAD, HEAD)], wkv_sem.at[h]) for h in range(4)]
+
+        def native(c):
+            src = wq_hbm.at[0, pl.ds(c * D, D)] if c < 8 else (wk_hbm if c < 10 else wv_hbm).at[0, pl.ds(c % 2 * D, D)]
+            return pltpu.make_async_copy(src, wg_v.at[:, pl.ds(c * HEAD, HEAD)], nat_sem.at[c])
+        natives = [native(c) for c in range(12)]
+        B = 256
+        per = B // C
+        blocks = half // B
+
+        def x_load(k):
+            part = (1 - k // blocks, pl.ds(k % blocks * per, per))
+            return pltpu.make_async_copy(x_hbm.at[part], ub.at[part], x_sem.at[k])
+        x_loads = [x_load(k) for k in range(2 * blocks)]
+        first = natives[8:] + x_loads[:1] + [load(4, tab_hbm.at[0], tab)] + x_loads[1:] + natives[:8]
     else:
         res_load = load(2, res_hbm, hb)
         first = [load(3, q_hbm, q_v), load(4, kv_hbm, kv)]
     for c in first:
         c.start()
-    for c in wo_tiles:
-        c.start()
-
-    @pl.when(is_end)
-    def _():
-        res_load.start()
-    wg_load.start()
     if layer == 1:
-        wu_load.start()
+        for c in wo_tiles:
+            c.start()
 
     bar = pltpu.get_barrier_semaphore()
 
-    @pl.when(z > 0)
-    def _():
-        pl.semaphore_signal(bar, inc=1, device_id=down, device_id_type=MESH)
-
-    @pl.when(z < 3)
-    def _():
-        pl.semaphore_signal(bar, inc=1, device_id=up, device_id_type=MESH)
-    if layer == 0:
-        for k in (1, 2, 3):
-            pl.semaphore_signal(bar, inc=1, device_id={'sp': lax.rem(s + k, 4)}, device_id_type=MESH)
-    pl.semaphore_wait(bar, jnp.where(is_end, 1, 2) + (3 if layer == 0 else 0))
+    peers = [{'tp': lax.rem(z + k, 4)} for k in (1, 2, 3)]
+    if layer == 0:
+        peers += [{'sp': lax.rem(s + k, 4)} for k in (1, 2, 3)]
+    for peer in peers:
+        pl.semaphore_signal(bar, inc=1, device_id=peer, device_id_type=MESH)
+    pl.semaphore_wait(bar, len(peers))
 
     kept = WD_KEPT[layer]
     flow = D // 256 - kept
@@ -141,16 +142,32 @@
         def tail(dst, kind):
             return pltpu.make_async_remote_copy(kv.at[2 * kind + dst // 2, pl.ds(rows, WINDOW), :], cache.at[kind],
                                                 tail_s.at[dst, kind], tail_r.at[kind], device_id={'sp': dst}, device_id_type=MESH)
-        B = 256
-        per = B // C
-        blocks = half // B
-        for c in first[:6]:
+        for p, group in enumerate((32, 128)):
+            row = lax.broadcasted_iota(jnp.int32, (256, 256), 0)
+            col = lax.broadcasted_iota(jnp.int32, (256, 256), 1)
+            perm[p] = jnp.where(col == lax.rem(row, group) * (256 // group) + row // group, 1.0, 0.0).astype(BF)
+
+        def by_head(p, block):
+            return jnp.dot(perm[p], block, preferred_element_type=F32).astype(BF)
+
+        for c in natives[8:]:
             c.wait()
+
+        def sort_kv(k, _):
+            for c in range(4):
+                w = by_head(1, wg_v[at(k * 256, 256), (8 + c) * HEAD:(9 + c) * HEAD])
+                for h in range(2):
+                    wkv_v[at(c % 2 * (D // 2) + k * 128, 128), (c // 2 * 2 + h) * HEAD:(c // 2 * 2 + h + 1) * HEAD] = w[h * 128:(h + 1) * 128]
+            return 0
+        lax.fori_loop(0, D // 256, sort_kv, 0, unroll=2)
+        load(4, tab_hbm.at[0], tab).wait()
 
         def kv_block(k, _):
             d = 1 - k // blocks
             i0 = lax.rem(k, blocks) * per
             row = d * half + i0 * C
+            part = ub.at[d, at(i0, per)]
+            pltpu.make_async_copy(part, part, x_sem.at[k]).wait()
 
             def norm(i, _):
                 ub[d, i0 + i] = rms(ub[d, i0 + i].astype(F32), g_ref[0, 0:1, :]).astype(BF)
@@ -176,10 +193,23 @@
                             tail(dst, kind).start()
             return 0
         lax.fori_loop(0, 2 * blocks, kv_block, 0)
-        for c in wkv_loads(1):
+        for c in natives[:8]:
+            c.wait()
+
+        def sort_q(k, _):
+            for c in range(8):
+                w = by_head(0, wg_v[at(k * 256, 256), c * HEAD:(c + 1) * HEAD])
+                for h in range(8):
+                    wu_v[at(c * (D // 8) + k * 32, 32), h * HEAD:(h + 1) * HEAD] = w[h * 32:(h + 1) * 32]
+            return 0
+        lax.fori_loop(0, D // 256, sort_q, 0)
+        for c in wo_tiles:
             c.start()
-        for c in wq_first:
-            c.wait()
+
+        @pl.when(is_end)
+        def _():
+            res_load.start()
+        wg_load.start()
 
         def q_block(k, _):
             d = k // blocks
@@ -194,17 +224,8 @@
                     for i in range(per):
                         q_v[d, i0 + i, c // 2, h * C:(h + 1) * C, :] = qe[i * C:(i + 1) * C]
             return 0
-        lax.fori_loop(0, 2 * blocks, q_block, 0)
-        wu_load.start()
-        load(4, tab_hbm.at[1], tab).start()
-
-    @pl.when(is_end)
-    def _():
-        res_load.wait()
-    for c in wd_loads:
-        c.start()
-    for k in range(WD_SLOTS):
-        wd_tile(k).start()
+        for d in range(2):
+            q_block(d * blocks, 0)
 
     def place(d, g, o):
         for h in range(4):
@@ -282,14 +303,81 @@
     else:
         for c in first:
             c.wait()
+
+        @pl.when(is_end)
+        def _():
+            res_load.start()
+        wg_load.start()
+        wu_load.start()
         y = s // 2
         caches = [pltpu.make_async_copy(kv.at[y], kc_hbm, c_sem.at[0]), pltpu.make_async_copy(kv.at[2 + y], vc_hbm, c_sem.at[1])]
         for c in caches:
             c.start()
         attend = attend_global
+    for c in wd_loads:
+        c.start()
+    for k in range(WD_SLOTS):
+        wd_tile(k).start()
+    if layer == 0:
+        def sort_in(k):
+            jobs = [pltpu.make_async_copy(wq_hbm.at[1, at(k * 1280, 1280)], qin, ri_sem.at[0])]
+            small = [pltpu.make_async_copy(w.at[1, at(k * 512, 512)], kvin.at[e], ri_sem.at[1 + e]) for e, w in enumerate((wk_hbm, wv_hbm))]
+            return jobs, small
+
+        def sort_out(k):
+            return (pltpu.make_async_copy(qo, wq1_hbm.at[:, at(k * 160, 160), :], ro_sem.at[0]),
+                    pltpu.make_async_copy(kvo, wkv1_hbm.at[:, at(k * 256, 256), :], ro_sem.at[1]))
+        q_parts, kv_parts = 8 * D // 1280, 2 * D // 512
+        for jobs in sort_in(0):
+            for c in jobs:
+                c.start()
+
+        def sort_next(t):
+            k = t - 1
+
+            @pl.when((k >= 1) & (k <= q_parts))
+            def _():
+                sort_out(k - 1)[0].wait()
+
+            @pl.when((k >= 1) & (k <= kv_parts))
+            def _():
+                sort_out(k - 1)[1].wait()
+
+            @pl.when((k >= 0) & (k < q_parts))
+            def _():
+                sort_in(k)[0][0].wait()
+                for e in range(5):
+                    w = by_head(0, qin[e * 256:(e + 1) * 256, :])
+                    for h in range(8):
+                        qo[h, e * 32:(e + 1) * 32, :] = w[h * 32:(h + 1) * 32]
+                sort_out(k)[0].start()
+
+                @pl.when(k + 1 < q_parts)
+                def _():
+                    sort_in(k + 1)[0][0].start()
+
+            @pl.when((k >= 0) & (k < kv_parts))
+            def _():
+                for c in sort_in(k)[1]:
+                    c.wait()
+                for e in range(2):
+                    for b in range(2):
+                        w = by_head(1, kvin[e, b * 256:(b + 1) * 256, :])
+                        for h in range(2):
+                            kvo[2 * e + h, b * 128:(b + 1) * 128, :] = w[h * 128:(h + 1) * 128]
+                sort_out(k)[1].start()
+
+                @pl.when(k + 1 < kv_parts)
+                def _():
+                    for c in sort_in(k + 1)[1]:
+                        c.start()
     attend(0)
     for c in wo_tiles:
         c.wait()
+
+    @pl.when(is_end)
+    def _():
+        res_load.wait()
 
     def red_copy(stage, recv, s_sem, r_sem, d, slot, i):
         k = lax.rem(i, RING)
@@ -300,11 +388,17 @@
         return pltpu.make_async_remote_copy(ub.at[d, i], ub.at[d, i], s_sem.at[d, i], r_sem.at[d, i],
                                             device_id=away[d], device_id_type=MESH)
 
+    def last_copy(d, hops):
+        i = n - 1
+        target = jnp.clip(z + hops if d == 0 else z - hops, 0, 3)
+        return pltpu.make_async_remote_copy(ub.at[d, i], ub.at[d, i], hx_sem.at[d, hops - 2], hr_sem.at[d, i],
+                                            device_id={'tp': target}, device_id_type=MESH)
+
     def out_copy(d, i):
         return pltpu.make_async_copy(ub.at[d, i], out_hbm.at[i] if layer == 0 else out_hbm.at[d, i], out_sem.at[d, i])
 
     if layer == 0:
-        wq_tiles = [pltpu.make_async_copy(wq_hbm.at[1, h], wa.at[pl.ds(h // 2 * D, D), pl.ds(h % 2 * HEAD, HEAD)], wq_sem.at[h]) for h in range(8)]
+        wq_tiles = [pltpu.make_async_copy(wq1_hbm.at[h], wa.at[pl.ds(h // 2 * D, D), pl.ds(h % 2 * HEAD, HEAD)], wq_sem.at[h]) for h in range(8)]
         pairs = n // 2
 
         def span_of(dev, d, k):
@@ -406,7 +500,7 @@
                 def _():
                     at_end(d, i)
 
-        def spread(s_sem, r_sem, first_tick, then):
+        def spread(s_sem, r_sem, first_tick, then, limit=n):
             for d in (0, 1):
                 i = t - first_tick - r[d]
                 act = (i >= 0) & (i < n) & (r[d] > 0)
@@ -415,7 +509,7 @@
                 def _():
                     cast_copy(s_sem, r_sem, d, i).wait_recv()
 
-                @pl.when(act & (r[d] < 3))
+                @pl.when(act & (r[d] < 3) & (i < limit))
                 def _():
                     cast_copy(s_sem, r_sem, d, i).start()
                 if then is not None:
@@ -447,6 +541,20 @@
         def _():
             attend(t + 1)
 
+        if layer == 0:
+            sort_next(t)
+
+            @pl.when(t < 2)
+            def _():
+                def later(k, _):
+                    return q_block(t * blocks + k, 0)
+                lax.fori_loop(1, blocks, later, 0)
+
+            @pl.when(t == 1)
+            def _():
+                wu_load.start()
+                load(4, tab_hbm.at[1], tab).start()
+
         @pl.when(t == 6)
         def _():
             for c in [wg_load, wu_load] + wd_loads:
@@ -501,20 +609,25 @@
         def m_end(d, i):
             ub[d, i] = (hb[i].astype(F32) + rms(sm[slot, d], g_ref[layer, 3:4, :])).astype(BF)
             cast_copy(hs_sem, hr_sem, d, i).start()
+
+            @pl.when(i == n - 1)
+            def _():
+                for hops in (2, 3):
+                    last_copy(d, hops).start()
             out_copy(d, i).start()
         reduce(sm, rm, ms_sem, mr_sem, 6, m_end)
-        spread(hs_sem, hr_sem, 9, None if layer == 0 else lambda d, i: out_copy(d, i).start())
+        spread(hs_sem, hr_sem, 9, None if layer == 0 else lambda d, i: out_copy(d, i).start(), n - 1)
 
         if layer == 0:
             @pl.when(t == n + 3)
             def _():
-                for c in wq_tiles:
+                for c in wkv_loads + wq_tiles:
                     c.start()
             first_qkv = n + 12 - pairs
 
             @pl.when(t == first_qkv)
             def _():
-                for c in wkv_loads(1) + [load(4, tab_hbm.at[1], tab)] + wq_tiles:
+                for c in wkv_loads + [load(4, tab_hbm.at[1], tab)] + wq_tiles:
                     c.wait()
 
             @pl.when(t >= first_qkv)
@@ -555,9 +668,14 @@
 
     def drain(i, _):
         for d in (0, 1):
-            @pl.when(r[d] < 3)
+            @pl.when((r[d] < 3) & ((i < n - 1) | (r[d] == 0)))
             def _():
                 cast_copy(hs_sem, hr_sem, d, i).wait_send()
+
+            @pl.when((r[d] == 0) & (i == n - 1))
+            def _():
+                for hops in (2, 3):
+                    last_copy(d, hops).wait_send()
             if layer == 0:
                 @pl.when(r[d] == 0)
                 def _():
@@ -568,6 +686,38 @@
     lax.fori_loop(0, n, drain, 0)
     for c in caches:
         c.wait()
+
+
+def finish_kernel(parts, *refs):
+    k = len(parts)
+    ins, outs, bufs, sems = refs[:k], refs[k:2 * k], refs[2 * k:3 * k], refs[3 * k:]
+    jobs = []
+    for p in range(k):
+        size = ins[p].shape[0] // parts[p]
+        for e in range(parts[p]):
+            cut = pl.ds(e * size, size)
+            jobs.append((pltpu.make_async_copy(ins[p].at[cut], bufs[p].at[cut], sems[0].at[len(jobs)]),
+                         pltpu.make_async_copy(bufs[p].at[cut], outs[p].at[cut], sems[1].at[len(jobs)])))
+    for job in jobs:
+        job[0].start()
+    for job in jobs:
+        job[0].wait()
+        job[1].start()
+    for job in jobs:
+        job[1].wait()
+
+
+def finish(arrays, parts):
+    any_ = pl.BlockSpec(memory_space=pl.ANY)
+    dma = pltpu.SemaphoreType.DMA
+    return pl.pallas_call(
+        functools.partial(finish_kernel, parts),
+        out_shape=[jax.ShapeDtypeStruct(a.shape, a.dtype) for a in arrays],
+        in_specs=[any_] * len(arrays), out_specs=[any_] * len(arrays),
+        scratch_shapes=[pltpu.VMEM(a.shape, a.dtype) for a in arrays] + [dma((sum(parts),)), dma((sum(parts),))],
+        compiler_params=pltpu.CompilerParams(vmem_limit_bytes=67043328),
+        name='finish',
+    )(*arrays)
 
 
 def run_layer(layer, heads, weights, out_shape):
@@ -586,15 +736,17 @@
         pltpu.VMEM((2, RING, C, D), F32), pltpu.VMEM((2, RING, C, D), F32),
         pltpu.VMEM((2 * C, ka), BF), pltpu.VMEM((2 * C, D), BF), pltpu.VMEM((2 * C, ff), BF),
         dma((7,)), dma((D // 256,)), dma((WD_KEPT[layer],)), dma((WD_SLOTS,)), dma((2, 2)), dma((2, RING)), dma((2, 2)), dma((2, RING)),
-        dma((2, n)), dma((2, n)), dma((2, n)), dma((2, n)), dma((2, n)), dma((2,))]
+        dma((2, n)), dma((2, n)), dma((2, n)), dma((2, n)), dma((2, 2)), dma((2, n)), dma((2,))]
     if layer == 0:
         p = n // 2
         scratch += [
             pltpu.VMEM((rows, HEAD), F32), pltpu.VMEM((D, 4 * HEAD), BF), pltpu.VMEM((4 * C, D), BF),
             pltpu.VMEM((2, 2, 2, 2, 4 * C, HEAD), BF), pltpu.VMEM((2, 2, 4, 2 * C, HEAD), BF), pltpu.VMEM((2, WINDOW, HEAD), BF),
-            dma((8,)), dma((4,)), dma, dma, dma((3, 2)), dma((2,)), dma((2, 2)), dma((2, p)), dma((2, 2)), dma((2, p)), dma((2, 2)),
+            pltpu.VMEM((2, 256, 256), BF), pltpu.VMEM((1280, HEAD), BF), pltpu.VMEM((2, 512, HEAD), BF),
+            pltpu.VMEM((8, 160, HEAD), BF), pltpu.VMEM((4, 256, HEAD), BF), dma((12,)), dma((3,)), dma((2,)),
+            dma((rows // 256,)), dma((8,)), dma((4,)), dma, dma, dma((3, 2)), dma((2,)), dma((2, 2)), dma((2, p)), dma((2, 2)), dma((2, p)), dma((2, 2)),
             dma((2, p)), dma((2, p)), dma((2, 2))]
-        in_specs = [any_, vmem] + [any_] * 3
+        in_specs = [any_, vmem] + [any_] * 4
     else:
         scratch += [pltpu.VMEM((2, 2, 3, 4 * C, HEAD), F32), pltpu.VMEM((2, 2, 2, 4 * C, KEYS), F32)]
         in_specs = [any_, any_, any_, vmem]
@@ -616,22 +768,26 @@
         rows = x.shape[0]
         n = rows // 2 // C
         shape = jax.ShapeDtypeStruct
-        heads_first = (0, 2, 1, 3)
-        wq = jnp.transpose(w_q, heads_first)
-        wkv = jnp.concatenate([jnp.transpose(w_k, heads_first), jnp.transpose(w_v, heads_first)], axis=1)
+        wq, wk, wv = (w.reshape(2, -1, HEAD) for w in (w_q, w_k, w_v))
         half = HEAD // 2
         freq = jnp.stack([base ** (-jnp.arange(half, dtype=F32) / half) for base in (LOCAL_BASE, GLOBAL_BASE)])
-        angles = pos.astype(F32)[None, :, None] * freq[:, None, :]
-        tab = jnp.concatenate([jnp.cos(angles), jnp.sin(angles)], axis=2)
+        grain = 32
+        coarse = pos.astype(F32)[::grain][None, :, None] * freq[:, None, :]
+        fine = jnp.arange(grain, dtype=F32)[None, :, None] * freq[:, None, :]
+        ca, sa, cb, sb = lax.optimization_barrier((jnp.cos(coarse), jnp.sin(coarse), jnp.cos(fine), jnp.sin(fine)))
+        ca, sa, cb, sb = ca[:, :, None], sa[:, :, None], cb[:, None], sb[:, None]
+        tab = jnp.concatenate([ca * cb - sa * sb, sa * cb + ca * sb], axis=3).reshape(2, rows, HEAD)
         weights = (w_o.reshape(2, 8 * HEAD, D), w_gate, w_up, w_down)
         qshape = shape((2, n, 2, 4 * C, HEAD), BF)
-        res, q1, kv1, kl, vl = run_layer(
-            0, (x.reshape(2, n, C, D), gains, tab, wq, wkv), weights,
-            [shape((n, C, D), BF), qshape, shape((4, 4 * rows, HEAD), BF), shape((WINDOW, HEAD), BF), shape((WINDOW, HEAD), BF)])
+        res, q1, kv1, kl, vl, _, _ = run_layer(
+            0, (x.reshape(2, n, C, D), gains, tab, wq, wk, wv), weights,
+            [shape((n, C, D), BF), qshape, shape((4, 4 * rows, HEAD), BF), shape((WINDOW, HEAD), BF), shape((WINDOW, HEAD), BF),
+             shape((8, D, HEAD), BF), shape((4, D, HEAD), BF)])
         out, kg, vg = run_layer(
             1, (res, q1, kv1, gains), weights,
             [shape((2, n, C, D), BF), shape((4 * rows, HEAD), BF), shape((4 * rows, HEAD), BF)])
-        return (out.reshape(rows, D), kl[:, None, :], vl[:, None, :], kg[:, None, :], vg[:, None, :])
+        out, kl, vl, kg, vg = finish((out.reshape(rows, D), kl, vl, kg, vg), (8, 1, 1, 2, 2))
+        return (out, kl[:, None, :], vl[:, None, :], kg[:, None, :], vg[:, None, :])
 
     token_spec = P(('rep', 'sp'), None)
     cache_spec = P('rep', ('tp', 'sp'), None)

time: 837 us -> 814 us (0.973)
  local copies, waits for them, and re-layouts: 19.1 us -> 0.11 us
    unnamed x18 -> x0, local copies, waits for them, and re-layouts: 18.4 us -> none
where the time goes in v3:
time: 814 us; the launch traced here: 809 us
  Pallas kernels  805 us (99%)
    pallas_call x2, Pallas kernels, run_layer(): pl.pallas_call(functools.partial(layer_kernel, layer), out_shape=out_shap...  799 us

profile of v3, /device:TPU:0, one launch (start us, length us, event | category | flops | bytes accessed | tf_op | source)
XLA Modules:
  0.0 809.0 jit_solution(1962123683731534004)
XLA Ops:
  0.7 0.7 convert_element_type.3
  1.4 0.1 slice.3
  1.5 0.3 fusion
  1.7 0.3 multiply_subtract_fusion
  2.0 1.3 pad_maximum_fusion.refs_2_
  3.4 414.7 %layer0.1 = (bf16[16,32,2560]{2,1,0:T(8,128)(2,1)}, bf16[2,16,2,128,128]{4,3,2,1,0:T(8,128)(2,1)}, bf16[4,4096,128]{2,1,0:T(8,128)(2,1)}, bf16[512,128]{1,0:T(8,...) custom-call(bf16[2,16,32,2560]{3,2,1,0:T(8,128)(2,1)} %bitcast.18, ...), custom_call_target="tpu_custom_call" | custom-call | flops 43620761600 | bytes 300000000 | tf_op jit(solution)/shard_map/layer0/pallas_call | solution.py:753
  418.1 384.5 %layer1.1 = (bf16[2,16,32,2560]{3,2,1,0:T(8,128)(2,1)}, bf16[4096,128]{1,0:T(8,128)(2,1)}, bf16[4096,128]{1,0:T(8,128)(2,1)}) custom-call(bf16[16,32,2560]{2,1,0:T(8,128)(2,1)} %get-tuple-element.26.refs_0_, bf16[2,16,2,128,128]{4,3,2,1,0:T(8,128)(2,1)} %get-tuple-element.27.refs_1_, bf16[4,4096,128]{2,1,0:T(8,128)(2,1)} %get-tuple-element.28.refs_2_, ...), custom_call_target="tpu_custom_call" | custom-call | flops 43620761600 | bytes 300000000 | tf_op jit(solution)/shard_map/layer1/pallas_call | solution.py:753
  802.6 6.1 finish.1
  (2 shorter events, 0.0 us)

commit v4 on v3

--- a/solution.py
+++ b/solution.py
@@ -159,7 +159,7 @@
                 for h in range(2):
                     wkv_v[at(c % 2 * (D // 2) + k * 128, 128), (c // 2 * 2 + h) * HEAD:(c // 2 * 2 + h + 1) * HEAD] = w[h * 128:(h + 1) * 128]
             return 0
-        lax.fori_loop(0, D // 256, sort_kv, 0, unroll=2)
+        lax.fori_loop(0, D // 256, sort_kv, 0, unroll=5)
         load(4, tab_hbm.at[0], tab).wait()
 
         def kv_block(k, _):
@@ -172,7 +172,7 @@
             def norm(i, _):
                 ub[d, i0 + i] = rms(ub[d, i0 + i].astype(F32), g_ref[0, 0:1, :]).astype(BF)
                 return 0
-            lax.fori_loop(0, per, norm, 0, unroll=2)
+            lax.fori_loop(0, per, norm, 0, unroll=4)
             p = jnp.dot(ub[d, at(i0, per)].reshape(B, D), wkv_v[...], preferred_element_type=F32)
             rope = rotor(tab[at(row, B), :])
             dst = at(WINDOW + row, B)
@@ -251,8 +251,16 @@
                 place(d, g, o / jnp.sum(p, axis=1, keepdims=True))
 
     def attend_global(t):
+        here = [(t - 3 + r[d] >= 0) & (t - 3 + r[d] < n) for d in range(2)]
+        both = here[0] & here[1]
+        for halves, cond in (((0, 1), both), ((0,), here[0] & ~both), ((1,), here[1] & ~both)):
+            @pl.when(cond)
+            def _():
+                attend_halves(t, halves)
+
+    def attend_halves(t, halves):
         ids = [chunk_at(t, d) for d in range(2)]
-        streams = [(d, g) for d in range(2) for g in range(2)]
+        streams = [(d, g) for d in halves for g in range(2)]
         for d, g in streams:
             st[d, g, 0] = jnp.full((4 * C, HEAD), -1e30, F32)
             st[d, g, 1] = jnp.zeros((4 * C, HEAD), F32)
@@ -286,12 +294,13 @@
                     update(e, d, g, 2 * j + e)
             return 0
         lax.fori_loop(0, s, two, 0)
-        for g in range(2):
-            score(1, 1, g, 2 * s + 1)
+        late = [(d, g) for d, g in streams if d == 1]
+        for d, g in late:
+            score(1, d, g, 2 * s + 1)
         for d, g in streams:
             update(0, d, g, 2 * s, masked=d == 0)
-        for g in range(2):
-            update(1, 1, g, 2 * s + 1, masked=True)
+        for d, g in late:
+            update(1, d, g, 2 * s + 1, masked=True)
         for d, g in streams:
             place(d, g, st[d, g, 2] / jnp.sum(st[d, g, 1], axis=1, keepdims=True))
 
@@ -313,6 +322,7 @@
         caches = [pltpu.make_async_copy(kv.at[y], kc_hbm, c_sem.at[0]), pltpu.make_async_copy(kv.at[2 + y], vc_hbm, c_sem.at[1])]
         for c in caches:
             c.start()
+        lhs_a[...] = jnp.zeros_like(lhs_a)
         attend = attend_global
     for c in wd_loads:
         c.start()
@@ -537,10 +547,6 @@
         reduce(so, ro, os_sem, or_sem, 0, o_end)
         spread(us_sem, ur_sem, 3, None)
 
-        @pl.when(t + 1 < n + 3)
-        def _():
-            attend(t + 1)
-
         if layer == 0:
             sort_next(t)
 
@@ -617,6 +623,10 @@
             out_copy(d, i).start()
         reduce(sm, rm, ms_sem, mr_sem, 6, m_end)
         spread(hs_sem, hr_sem, 9, None if layer == 0 else lambda d, i: out_copy(d, i).start(), n - 1)
+
+        @pl.when(t + 1 < n + 3)
+        def _():
+            attend(t + 1)
 
         if layer == 0:
             @pl.when(t == n + 3)

time: 814 us -> 812 us (level)
  no operation moved by 1% of the time
where the time goes in v4:
time: 812 us; the launch traced here: 809 us
  Pallas kernels  805 us (99%)
    pallas_call x2, Pallas kernels, run_layer(): pl.pallas_call(functools.partial(layer_kernel, layer), out_shape=out_shap...  799 us

profile of v4, /device:TPU:0, one launch (start us, length us, event | category | flops | bytes accessed | tf_op | source)
XLA Modules:
  0.0 808.5 jit_solution(2157682815416899425)
XLA Ops:
  0.7 0.7 convert_element_type.3
  1.4 0.1 slice.3
  1.5 0.3 fusion
  1.7 0.3 multiply_subtract_fusion
  2.0 1.3 pad_maximum_fusion.refs_2_
  3.4 412.8 %layer0.1 = (bf16[16,32,2560]{2,1,0:T(8,128)(2,1)}, bf16[2,16,2,128,128]{4,3,2,1,0:T(8,128)(2,1)}, bf16[4,4096,128]{2,1,0:T(8,128)(2,1)}, bf16[512,128]{1,0:T(8,...) custom-call(bf16[2,16,32,2560]{3,2,1,0:T(8,128)(2,1)} %bitcast.18, ...), custom_call_target="tpu_custom_call" | custom-call | flops 43620761600 | bytes 300000000 | tf_op jit(solution)/shard_map/layer0/pallas_call | solution.py:763
  416.2 386.0 %layer1.1 = (bf16[2,16,32,2560]{3,2,1,0:T(8,128)(2,1)}, bf16[4096,128]{1,0:T(8,128)(2,1)}, bf16[4096,128]{1,0:T(8,128)(2,1)}) custom-call(bf16[16,32,2560]{2,1,0:T(8,128)(2,1)} %get-tuple-element.26.refs_0_, bf16[2,16,2,128,128]{4,3,2,1,0:T(8,128)(2,1)} %get-tuple-element.27.refs_1_, bf16[4,4096,128]{2,1,0:T(8,128)(2,1)} %get-tuple-element.28.refs_2_, ...), custom_call_target="tpu_custom_call" | custom-call | flops 43620761600 | bytes 300000000 | tf_op jit(solution)/shard_map/layer1/pallas_call | solution.py:763
  802.2 6.1 finish.1
  (2 shorter events, 0.0 us)
